TPU v7x, 32 devices: a whole 2x2x4 slice. The times are simulated.
32 devices in a mesh: band: 2 (over core), lane: 16 (over z, y, x).
Axes of the slice: x: 2, y: 2, z: 4, core: 2. Of those that a mesh axis runs over, the one named last changes fastest.
Arguments:
- load_terms: float32 [128, 1024, 128], P('band', 'lane'), may hold values from -6 to 6
- start_values: float32 [128, 1024, 128], P('band', 'lane'), may hold values from -6 to 6
- reaction_rate: float32 [128, 1024, 128], P('band', 'lane'), may hold values from 0.1 to 0.9
Outputs:
- solution: float32 [128, 1024, 128], P('band', 'lane')
All inputs are finite; a program needn't handle non-finite values.
Results may differ from a plain program's by a relative error of at most 0.0003.
Values sent between devices are 32-bit elements.
A program may use at most 64 MiB of HBM per device.

v0:
```python
import jax
import jax.numpy as jnp
from jax import lax
from jax.sharding import PartitionSpec as P

RATIO = 4
BEFORE = 3
AFTER = 2
INNER = 13


def extended(cells, sides, width, closed):
    for axis, dim in sides:
        count = lax.axis_size(axis)
        ends = count if closed else count - 1
        head = lax.slice_in_dim(cells, 0, width, axis=dim)
        tail = lax.slice_in_dim(cells, cells.shape[dim] - width, cells.shape[dim], axis=dim)
        cells = jnp.concatenate(
            [
                lax.ppermute(tail, axis, [(i, (i + 1) % count) for i in range(ends)]),
                cells,
                lax.ppermute(head, axis, [((i + 1) % count, i) for i in range(ends)]),
            ],
            axis=dim,
        )
    return cells


def cross_sum(padded):
    inner_y, inner_x = (padded.shape[0] - 2, padded.shape[1] - 2)
    middle_rows = lax.slice_in_dim(padded, 1, 1 + inner_y, axis=0)
    middle_columns = lax.slice_in_dim(padded, 1, 1 + inner_x, axis=1)
    return (
        lax.slice_in_dim(middle_columns, 0, inner_y, axis=0)
        + lax.slice_in_dim(middle_columns, 2, 2 + inner_y, axis=0)
        + lax.slice_in_dim(middle_rows, 0, inner_x, axis=1)
        + lax.slice_in_dim(middle_rows, 2, 2 + inner_x, axis=1)
    )


def smooth_step(padded, values, load, mass_here):
    return values + 0.8 * (load + cross_sum(padded) - (4.0 + mass_here) * values) / (
        4.0 + mass_here
    )


def block_means(values):
    cut = values.reshape(
        values.shape[0] // RATIO, RATIO, values.shape[1] // RATIO, RATIO, values.shape[2]
    )
    return jnp.mean(cut, axis=(1, 3))


def spread_blocks(values):
    return jnp.repeat(jnp.repeat(values, RATIO, axis=0), RATIO, axis=1)


def without_rim(values):
    return lax.slice_in_dim(
        lax.slice_in_dim(values, 1, values.shape[0] - 1, axis=0), 1, values.shape[1] - 1, axis=1
    )


def shards(load_terms, start_values, reaction_rate):
    values = start_values
    for sweep in range(BEFORE):
        values = smooth_step(
            extended(values, (("band", 0), ("lane", 1)), 1, True), values, load_terms, reaction_rate
        )
    defect = (
        load_terms
        + cross_sum(extended(values, (("band", 0), ("lane", 1)), 1, True))
        - (4.0 + reaction_rate) * values
    )
    coarse_load, coarse_mass = (block_means(defect) * RATIO, block_means(reaction_rate) * RATIO)
    coarse_values = 0.8 * coarse_load / (4.0 + coarse_mass)
    load_mass = extended(
        jnp.concatenate([coarse_load, coarse_mass], axis=2), (("band", 0), ("lane", 1)), 2, True
    )
    wide_load, wide_mass = jnp.split(load_mass, 2, axis=2)
    for group in range((INNER - 1) // 2):
        wide_values = extended(coarse_values, (("band", 0), ("lane", 1)), 2, True)
        once = smooth_step(
            wide_values, without_rim(wide_values), without_rim(wide_load), without_rim(wide_mass)
        )
        middle = without_rim(once)
        coarse_values = smooth_step(once, middle, coarse_load, coarse_mass)
    values = values + spread_blocks(coarse_values)
    for sweep in range(AFTER):
        values = smooth_step(
            extended(values, (("band", 0), ("lane", 1)), 1, True), values, load_terms, reaction_rate
        )
    solution = values
    return solution


def solution(mesh):
    return jax.shard_map(
        shards,
        mesh=mesh,
        in_specs=(P("band", "lane", None), P("band", "lane", None), P("band", "lane", None)),
        out_specs=P("band", "lane", None),
        check_vma=False,
    )
```

profile of v0, /device:TPU:0, one launch (start us, length us, event | category | flops | bytes accessed | tf_op | source)
XLA Modules:
  0.0 153.7 jit_solution(12387492120210697072)
XLA Ops:
  0.0 0.8 fusion.125
  1.4 0.8 collective-permute-done
  2.2 2.0 %constant_dynamic-update-slice_fusion.1 = f32[66,64,128]{2,1,0:T(8,128)S(1)} fusion(f32[66,64,128]{2,1,0:T(8,128)S(1)} %constant_dynamic-update-slice_fusion.2, f32[64,64,128]{2,1,0:T(8,128)} %param.4), kind=kLoop, calls=%fused_computation.277 | loop fusion | bytes 4194304
  4.2 2.9 %collective-permute-start.2 = (f32[66,1,128]{2,1,0:T(1,128)S(1)}, f32[66,1,128]{2,1,0:T(1,128)S(1)}, u32[]{:S(2)}, u32[]{:S(2)}) collective-permute-start(f32[66,1,128]{2,1,0:T(1,128)S(1)} %get-tuple-element.18), channel_id=1, source_target_pairs={{0,1},{1,2},{2,3},{3,4},{4,5},{5,6},{6,7},{7,8},{8,9},{9,10},{10,1... | collective-permute-start | bytes 101384 | tf_op jit(solution)/shard_map/ppermute | solution.py:20
  7.1 4.1 %collective-permute-start.3 = (f32[66,1,128]{2,1,0:T(1,128)S(1)}, f32[66,1,128]{2,1,0:T(1,128)S(1)}, u32[]{:S(2)}, u32[]{:S(2)}) collective-permute-start(f32[66,1,128]{2,1,0:T(1,128)S(1)} %get-tuple-element.19), channel_id=1, source_target_pairs={{1,0},{2,1},{3,2},{4,3},{5,4},{6,5},{7,6},{8,7},{9,8},{10,9},{11,1... | collective-permute-start | bytes 101384 | tf_op jit(solution)/shard_map/ppermute | solution.py:22
  11.2 1.8 %collective-permute-done.2 = f32[66,1,128]{2,1,0:T(1,128)S(1)} collective-permute-done((f32[66,1,128]{2,1,0:T(1,128)S(1)}, f32[66,1,128]{2,1,0:T(1,128)S(1)}, u32[]{:S(2)}, u32[]{:S(2)}) %collective-permute-start.2) | collective-permute-done | bytes 33824 | tf_op jit(solution)/shard_map/ppermute | solution.py:20
  13.0 5.7 %fusion.42 = f32[64,64,128]{2,1,0:T(8,128)S(1)} fusion(f32[64,64,128]{2,1,0:T(8,128)} %param.4, f32[64,64,128]{2,1,0:T(8,128)S(1)} %copy-done.1, f32[66,1,128]{2,1,0:T(1,128)S(1)} %collective-permute-done.3, f32[66,64,128]{2,1,0:T(8,128)S(1)} %constant_dynamic-update-slice_fusion, f32[66,1,128]{2,1,0:T(1,128)S(1)} %collective-permute-done.2, ...), kind=kLoop, calls=%fused_computation.83 | loop fusion | flops 7340032 | bytes 10684416 | tf_op jit(solution)/shard_map/add | solution.py:42
  19.4 0.7 collective-permute-done.4
  20.7 5.3 %collective-permute-start.7 = (f32[66,1,128]{2,1,0:T(1,128)S(1)}, f32[66,1,128]{2,1,0:T(1,128)S(1)}, u32[]{:S(2)}, u32[]{:S(2)}) collective-permute-start(f32[66,1,128]{2,1,0:T(1,128)S(1)} %get-tuple-element.17), channel_id=1, source_target_pairs={{1,0},{2,1},{3,2},{4,3},{5,4},{6,5},{7,6},{8,7},{9,8},{10,9},{11,1... | collective-permute-start | bytes 101384 | tf_op jit(solution)/shard_map/ppermute | solution.py:22
  26.1 1.9 %collective-permute-done.6 = f32[66,1,128]{2,1,0:T(1,128)S(1)} collective-permute-done((f32[66,1,128]{2,1,0:T(1,128)S(1)}, f32[66,1,128]{2,1,0:T(1,128)S(1)}, u32[]{:S(2)}, u32[]{:S(2)}) %collective-permute-start.6) | collective-permute-done | bytes 33824 | tf_op jit(solution)/shard_map/ppermute | solution.py:20
  27.9 3.4 %fusion.34 = f32[64,64,128]{2,1,0:T(8,128)S(1)} fusion(f32[64,64,128]{2,1,0:T(8,128)S(1)} %fusion.42, f32[64,64,128]{2,1,0:T(8,128)S(1)} %copy-done.1, f32[66,1,128]{2,1,0:T(1,128)S(1)} %collective-permute-done.7, f32[1,64,128]{2,1,0:T(8,128)S(1)} %collective-permute-done.5, f32[1,64,128]{2,1,0:T(8,128)S(1)} %collective-permute-done.4, ...), kind=kLoop, calls=%fused_computation.67 | loop fusion | flops 9437184 | bytes 8521728 | tf_op jit(solution)/shard_map/add | solution.py:42
  31.9 0.7 collective-permute-done.8
  32.9 5.7 %collective-permute-start.11 = (f32[66,1,128]{2,1,0:T(1,128)S(1)}, f32[66,1,128]{2,1,0:T(1,128)S(1)}, u32[]{:S(2)}, u32[]{:S(2)}) collective-permute-start(f32[66,1,128]{2,1,0:T(1,128)S(1)} %get-tuple-element.15), channel_id=1, source_target_pairs={{1,0},{2,1},{3,2},{4,3},{5,4},{6,5},{7,6},{8,7},{9,8},{10,9},{11,1... | collective-permute-start | bytes 101384 | tf_op jit(solution)/shard_map/ppermute | solution.py:22
  38.6 1.9 %collective-permute-done.10 = f32[66,1,128]{2,1,0:T(1,128)S(1)} collective-permute-done((f32[66,1,128]{2,1,0:T(1,128)S(1)}, f32[66,1,128]{2,1,0:T(1,128)S(1)}, u32[]{:S(2)}, u32[]{:S(2)}) %collective-permute-start.10) | collective-permute-done | bytes 33824 | tf_op jit(solution)/shard_map/ppermute | solution.py:20
  40.5 3.4 %fusion.26 = f32[64,64,128]{2,1,0:T(8,128)S(1)} fusion(f32[64,64,128]{2,1,0:T(8,128)S(1)} %fusion.34, f32[64,64,128]{2,1,0:T(8,128)S(1)} %copy-done.1, f32[66,1,128]{2,1,0:T(1,128)S(1)} %collective-permute-done.11, f32[1,64,128]{2,1,0:T(8,128)S(1)} %collective-permute-done.9, f32[1,64,128]{2,1,0:T(8,128)S(1)} %collective-permute-done.8, ...), kind=kLoop, calls=%fused_computation.51 | loop fusion | flops 9437184 | bytes 8521728 | tf_op jit(solution)/shard_map/add | solution.py:42
  44.5 0.7 collective-permute-done.12
  45.4 5.7 %collective-permute-start.15 = (f32[66,1,128]{2,1,0:T(1,128)S(1)}, f32[66,1,128]{2,1,0:T(1,128)S(1)}, u32[]{:S(2)}, u32[]{:S(2)}) collective-permute-start(f32[66,1,128]{2,1,0:T(1,128)S(1)} %get-tuple-element.13), channel_id=1, source_target_pairs={{1,0},{2,1},{3,2},{4,3},{5,4},{6,5},{7,6},{8,7},{9,8},{10,9},{11,1... | collective-permute-start | bytes 101384 | tf_op jit(solution)/shard_map/ppermute | solution.py:22
  51.2 0.7 reduce_sum.19
  51.8 1.2 collective-permute-done.14
  53.0 9.1 %fusion.18 = f32[64,64,128]{2,1,0:T(8,128)} fusion(f32[64,64,128]{2,1,0:T(8,128)} %param.3, f32[66,1,128]{2,1,0:T(1,128)S(1)} %collective-permute-done.15, f32[1,64,128]{2,1,0:T(8,128)S(1)} %collective-permute-done.13, f32[64,64,128]{2,1,0:T(8,128)} %copy-done.3, f32[1,64,128]{2,1,0:T(8,128)S(1)} %collective-permute-done.12, ...), kind=kLoop, calls=%fused_computation.35 | loop fusion | flops 7864320 | bytes 8521728 | tf_op jit(solution)/shard_map/sub | solution.py:71
  62.1 2.3 %reduce_sum.18 = f32[16,16,128]{2,1,0:T(8,128)S(1)} reduce(f32[16,4,16,4,128]{4,3,2,1,0:T(4,128)} %bitcast.6, f32[]{:T(128)} %constant.7.clone.1), dimensions={1,3}, to_apply=%region_0.0 | reduce | flops 491520 | bytes 2228228 | tf_op jit(solution)/shard_map/reduce_sum | solution.py:51
  65.9 5.7 %collective-permute-start.19 = (f32[20,2,128]{2,1,0:T(2,128)S(1)}, f32[20,2,128]{2,1,0:T(2,128)S(1)}, u32[]{:S(2)}, u32[]{:S(2)}) collective-permute-start(f32[20,2,128]{2,1,0:T(2,128)S(1)} %get-tuple-element.47), channel_id=1, source_target_pairs={{1,0},{2,1},{3,2},{4,3},{5,4},{6,5},{7,6},{8,7},{9,8},{10,9},{11,1... | collective-permute-start | bytes 61448 | tf_op jit(solution)/shard_map/ppermute | solution.py:22
  71.7 5.6 %collective-permute-start.23 = (f32[20,2,256]{2,1,0:T(2,128)S(1)}, f32[20,2,256]{2,1,0:T(2,128)S(1)}, u32[]{:S(2)}, u32[]{:S(2)}) collective-permute-start(f32[20,2,256]{2,1,0:T(2,128)S(1)} %get-tuple-element.33), channel_id=1, source_target_pairs={{1,0},{2,1},{3,2},{4,3},{5,4},{6,5},{7,6},{8,7},{9,8},{10,9},{11,1... | collective-permute-start | bytes 122888 | tf_op jit(solution)/shard_map/ppermute | solution.py:22
  77.4 1.9 %collective-permute-done.22 = f32[20,2,256]{2,1,0:T(2,128)S(1)} collective-permute-done((f32[20,2,256]{2,1,0:T(2,128)S(1)}, f32[20,2,256]{2,1,0:T(2,128)S(1)}, u32[]{:S(2)}, u32[]{:S(2)}) %collective-permute-start.22) | collective-permute-done | bytes 40992 | tf_op jit(solution)/shard_map/ppermute | solution.py:20
  80.2 0.7 collective-permute-done.24
  81.1 5.7 %collective-permute-start.27 = (f32[20,2,128]{2,1,0:T(2,128)S(1)}, f32[20,2,128]{2,1,0:T(2,128)S(1)}, u32[]{:S(2)}, u32[]{:S(2)}) collective-permute-start(f32[20,2,128]{2,1,0:T(2,128)S(1)} %get-tuple-element.45), channel_id=1, source_target_pairs={{1,0},{2,1},{3,2},{4,3},{5,4},{6,5},{7,6},{8,7},{9,8},{10,9},{11,1... | collective-permute-start | bytes 61448 | tf_op jit(solution)/shard_map/ppermute | solution.py:22
  86.8 1.7 %collective-permute-done.26 = f32[20,2,128]{2,1,0:T(2,128)S(1)} collective-permute-done((f32[20,2,128]{2,1,0:T(2,128)S(1)}, f32[20,2,128]{2,1,0:T(2,128)S(1)}, u32[]{:S(2)}, u32[]{:S(2)}) %collective-permute-start.26) | collective-permute-done | bytes 20512 | tf_op jit(solution)/shard_map/ppermute | solution.py:20
  89.3 0.7 collective-permute-done.28
  90.3 5.9 %collective-permute-start.31 = (f32[20,2,128]{2,1,0:T(2,128)S(1)}, f32[20,2,128]{2,1,0:T(2,128)S(1)}, u32[]{:S(2)}, u32[]{:S(2)}) collective-permute-start(f32[20,2,128]{2,1,0:T(2,128)S(1)} %get-tuple-element.43), channel_id=1, source_target_pairs={{1,0},{2,1},{3,2},{4,3},{5,4},{6,5},{7,6},{8,7},{9,8},{10,9},{11,1... | collective-permute-start | bytes 61448 | tf_op jit(solution)/shard_map/ppermute | solution.py:22
  96.2 1.5 collective-permute-done.30
  98.5 0.7 collective-permute-done.32
  99.5 5.9 %collective-permute-start.35 = (f32[20,2,128]{2,1,0:T(2,128)S(1)}, f32[20,2,128]{2,1,0:T(2,128)S(1)}, u32[]{:S(2)}, u32[]{:S(2)}) collective-permute-start(f32[20,2,128]{2,1,0:T(2,128)S(1)} %get-tuple-element.41), channel_id=1, source_target_pairs={{1,0},{2,1},{3,2},{4,3},{5,4},{6,5},{7,6},{8,7},{9,8},{10,9},{11,1... | collective-permute-start | bytes 61448 | tf_op jit(solution)/shard_map/ppermute | solution.py:22
  105.4 1.7 %collective-permute-done.34 = f32[20,2,128]{2,1,0:T(2,128)S(1)} collective-permute-done((f32[20,2,128]{2,1,0:T(2,128)S(1)}, f32[20,2,128]{2,1,0:T(2,128)S(1)}, u32[]{:S(2)}, u32[]{:S(2)}) %collective-permute-start.34) | collective-permute-done | bytes 20512 | tf_op jit(solution)/shard_map/ppermute | solution.py:20
  107.9 0.7 collective-permute-done.36
  108.8 5.7 %collective-permute-start.39 = (f32[20,2,128]{2,1,0:T(2,128)S(1)}, f32[20,2,128]{2,1,0:T(2,128)S(1)}, u32[]{:S(2)}, u32[]{:S(2)}) collective-permute-start(f32[20,2,128]{2,1,0:T(2,128)S(1)} %get-tuple-element.39), channel_id=1, source_target_pairs={{1,0},{2,1},{3,2},{4,3},{5,4},{6,5},{7,6},{8,7},{9,8},{10,9},{11,1... | collective-permute-start | bytes 61448 | tf_op jit(solution)/shard_map/ppermute | solution.py:22
  114.6 1.7 %collective-permute-done.38 = f32[20,2,128]{2,1,0:T(2,128)S(1)} collective-permute-done((f32[20,2,128]{2,1,0:T(2,128)S(1)}, f32[20,2,128]{2,1,0:T(2,128)S(1)}, u32[]{:S(2)}, u32[]{:S(2)}) %collective-permute-start.38) | collective-permute-done | bytes 20512 | tf_op jit(solution)/shard_map/ppermute | solution.py:20
  117.1 0.7 collective-permute-done.40
  118.1 5.7 %collective-permute-start.43 = (f32[20,2,128]{2,1,0:T(2,128)S(1)}, f32[20,2,128]{2,1,0:T(2,128)S(1)}, u32[]{:S(2)}, u32[]{:S(2)}) collective-permute-start(f32[20,2,128]{2,1,0:T(2,128)S(1)} %get-tuple-element.37), channel_id=1, source_target_pairs={{1,0},{2,1},{3,2},{4,3},{5,4},{6,5},{7,6},{8,7},{9,8},{10,9},{11,1... | collective-permute-start | bytes 61448 | tf_op jit(solution)/shard_map/ppermute | solution.py:22
  123.8 1.7 %collective-permute-done.42 = f32[20,2,128]{2,1,0:T(2,128)S(1)} collective-permute-done((f32[20,2,128]{2,1,0:T(2,128)S(1)}, f32[20,2,128]{2,1,0:T(2,128)S(1)}, u32[]{:S(2)}, u32[]{:S(2)}) %collective-permute-start.42) | collective-permute-done | bytes 20512 | tf_op jit(solution)/shard_map/ppermute | solution.py:20
  126.4 0.9 copy-done.4
  128.3 0.7 collective-permute-done.44
  129.2 5.7 %collective-permute-start.47 = (f32[66,1,128]{2,1,0:T(1,128)S(1)}, f32[66,1,128]{2,1,0:T(1,128)S(1)}, u32[]{:S(2)}, u32[]{:S(2)}) collective-permute-start(f32[66,1,128]{2,1,0:T(1,128)S(1)} %get-tuple-element.11), channel_id=1, source_target_pairs={{1,0},{2,1},{3,2},{4,3},{5,4},{6,5},{7,6},{8,7},{9,8},{10,9},{11,1... | collective-permute-start | bytes 101384 | tf_op jit(solution)/shard_map/ppermute | solution.py:22
  135.0 1.9 %collective-permute-done.46 = f32[66,1,128]{2,1,0:T(1,128)S(1)} collective-permute-done((f32[66,1,128]{2,1,0:T(1,128)S(1)}, f32[66,1,128]{2,1,0:T(1,128)S(1)}, u32[]{:S(2)}, u32[]{:S(2)}) %collective-permute-start.46) | collective-permute-done | bytes 33824 | tf_op jit(solution)/shard_map/ppermute | solution.py:20
  136.8 3.4 %fusion.13 = f32[64,64,128]{2,1,0:T(8,128)S(1)} fusion(f32[64,64,128]{2,1,0:T(8,128)S(1)} %add.394, f32[64,64,128]{2,1,0:T(8,128)S(1)} %copy-done.2, f32[66,1,128]{2,1,0:T(1,128)S(1)} %collective-permute-done.47, f32[1,64,128]{2,1,0:T(8,128)S(1)} %collective-permute-done.45, f32[1,64,128]{2,1,0:T(8,128)S(1)} %collective-permute-done.44, ...), kind=kLoop, calls=%fused_computation.22 | loop fusion | flops 9437184 | bytes 8521728 | tf_op jit(solution)/shard_map/add | solution.py:42
  140.8 0.7 collective-permute-done.48
  141.8 5.7 %collective-permute-start.51 = (f32[66,1,128]{2,1,0:T(1,128)S(1)}, f32[66,1,128]{2,1,0:T(1,128)S(1)}, u32[]{:S(2)}, u32[]{:S(2)}) collective-permute-start(f32[66,1,128]{2,1,0:T(1,128)S(1)} %get-tuple-element.9), channel_id=1, source_target_pairs={{1,0},{2,1},{3,2},{4,3},{5,4},{6,5},{7,6},{8,7},{9,8},{10,9},{11,1... | collective-permute-start | bytes 101384 | tf_op jit(solution)/shard_map/ppermute | solution.py:22
  147.5 1.9 %collective-permute-done.50 = f32[66,1,128]{2,1,0:T(1,128)S(1)} collective-permute-done((f32[66,1,128]{2,1,0:T(1,128)S(1)}, f32[66,1,128]{2,1,0:T(1,128)S(1)}, u32[]{:S(2)}, u32[]{:S(2)}) %collective-permute-start.50) | collective-permute-done | bytes 33824 | tf_op jit(solution)/shard_map/ppermute | solution.py:20
  149.4 4.3 %fusion.5 = f32[64,64,128]{2,1,0:T(8,128)} fusion(f32[64,64,128]{2,1,0:T(8,128)S(1)} %fusion.13, f32[64,64,128]{2,1,0:T(8,128)S(1)} %copy-done.2, f32[66,1,128]{2,1,0:T(1,128)S(1)} %collective-permute-done.51, f32[1,64,128]{2,1,0:T(8,128)S(1)} %collective-permute-done.49, f32[1,64,128]{2,1,0:T(8,128)S(1)} %collective-permute-done.48, ...), kind=kLoop, calls=%fused_computation.6 | loop fusion | flops 9437184 | bytes 8521728 | tf_op jit(solution)/shard_map/add | solution.py:42
  (125 shorter events, 13.6 us)
Async XLA Ops:
  0.8 1.4 collective-permute-start
  1.3 2.9 %collective-permute-start.1 = (f32[1,64,128]{2,1,0:T(8,128)S(1)}, f32[1,64,128]{2,1,0:T(8,128)S(1)}, u32[]{:S(2)}, u32[]{:S(2)}) collective-permute-start(f32[1,64,128]{2,1,0:T(8,128)S(1)} %get-tuple-element.30), channel_id=1, source_target_pairs={{16,0},{0,16},{17,1},{1,17},{18,2},{2,18},{19,3},{3,19},{20,4},{4,... | collective-permute-start | bytes 98312 | tf_op jit(solution)/shard_map/ppermute | solution.py:22
  4.2 8.8 %collective-permute-start.2 = (f32[66,1,128]{2,1,0:T(1,128)S(1)}, f32[66,1,128]{2,1,0:T(1,128)S(1)}, u32[]{:S(2)}, u32[]{:S(2)}) collective-permute-start(f32[66,1,128]{2,1,0:T(1,128)S(1)} %get-tuple-element.18), channel_id=1, source_target_pairs={{0,1},{1,2},{2,3},{3,4},{4,5},{5,6},{6,7},{7,8},{8,9},{9,10},{10,1... | collective-permute-start | bytes 101384 | tf_op jit(solution)/shard_map/ppermute | solution.py:20
  7.1 5.9 %collective-permute-start.3 = (f32[66,1,128]{2,1,0:T(1,128)S(1)}, f32[66,1,128]{2,1,0:T(1,128)S(1)}, u32[]{:S(2)}, u32[]{:S(2)}) collective-permute-start(f32[66,1,128]{2,1,0:T(1,128)S(1)} %get-tuple-element.19), channel_id=1, source_target_pairs={{1,0},{2,1},{3,2},{4,3},{5,4},{6,5},{7,6},{8,7},{9,8},{10,9},{11,1... | collective-permute-start | bytes 101384 | tf_op jit(solution)/shard_map/ppermute | solution.py:22
  18.8 1.3 collective-permute-start.4
  18.9 1.4 collective-permute-start.5
  20.3 7.6 %collective-permute-start.6 = (f32[66,1,128]{2,1,0:T(1,128)S(1)}, f32[66,1,128]{2,1,0:T(1,128)S(1)}, u32[]{:S(2)}, u32[]{:S(2)}) collective-permute-start(f32[66,1,128]{2,1,0:T(1,128)S(1)} %get-tuple-element.16), channel_id=1, source_target_pairs={{0,1},{1,2},{2,3},{3,4},{4,5},{5,6},{6,7},{7,8},{8,9},{9,10},{10,1... | collective-permute-start | bytes 101384 | tf_op jit(solution)/shard_map/ppermute | solution.py:20
  20.7 7.2 %collective-permute-start.7 = (f32[66,1,128]{2,1,0:T(1,128)S(1)}, f32[66,1,128]{2,1,0:T(1,128)S(1)}, u32[]{:S(2)}, u32[]{:S(2)}) collective-permute-start(f32[66,1,128]{2,1,0:T(1,128)S(1)} %get-tuple-element.17), channel_id=1, source_target_pairs={{1,0},{2,1},{3,2},{4,3},{5,4},{6,5},{7,6},{8,7},{9,8},{10,9},{11,1... | collective-permute-start | bytes 101384 | tf_op jit(solution)/shard_map/ppermute | solution.py:22
  31.3 1.3 collective-permute-start.8
  31.4 1.4 collective-permute-start.9
  32.8 7.6 %collective-permute-start.10 = (f32[66,1,128]{2,1,0:T(1,128)S(1)}, f32[66,1,128]{2,1,0:T(1,128)S(1)}, u32[]{:S(2)}, u32[]{:S(2)}) collective-permute-start(f32[66,1,128]{2,1,0:T(1,128)S(1)} %get-tuple-element.14), channel_id=1, source_target_pairs={{0,1},{1,2},{2,3},{3,4},{4,5},{5,6},{6,7},{7,8},{8,9},{9,10},{10,1... | collective-permute-start | bytes 101384 | tf_op jit(solution)/shard_map/ppermute | solution.py:20
  32.9 7.6 %collective-permute-start.11 = (f32[66,1,128]{2,1,0:T(1,128)S(1)}, f32[66,1,128]{2,1,0:T(1,128)S(1)}, u32[]{:S(2)}, u32[]{:S(2)}) collective-permute-start(f32[66,1,128]{2,1,0:T(1,128)S(1)} %get-tuple-element.15), channel_id=1, source_target_pairs={{1,0},{2,1},{3,2},{4,3},{5,4},{6,5},{7,6},{8,7},{9,8},{10,9},{11,1... | collective-permute-start | bytes 101384 | tf_op jit(solution)/shard_map/ppermute | solution.py:22
  43.9 1.3 collective-permute-start.12
  44.0 1.4 collective-permute-start.13
  45.4 7.6 %collective-permute-start.14 = (f32[66,1,128]{2,1,0:T(1,128)S(1)}, f32[66,1,128]{2,1,0:T(1,128)S(1)}, u32[]{:S(2)}, u32[]{:S(2)}) collective-permute-start(f32[66,1,128]{2,1,0:T(1,128)S(1)} %get-tuple-element.12), channel_id=1, source_target_pairs={{0,1},{1,2},{2,3},{3,4},{4,5},{5,6},{6,7},{7,8},{8,9},{9,10},{10,1... | collective-permute-start | bytes 101384 | tf_op jit(solution)/shard_map/ppermute | solution.py:20
  45.4 7.6 %collective-permute-start.15 = (f32[66,1,128]{2,1,0:T(1,128)S(1)}, f32[66,1,128]{2,1,0:T(1,128)S(1)}, u32[]{:S(2)}, u32[]{:S(2)}) collective-permute-start(f32[66,1,128]{2,1,0:T(1,128)S(1)} %get-tuple-element.13), channel_id=1, source_target_pairs={{1,0},{2,1},{3,2},{4,3},{5,4},{6,5},{7,6},{8,7},{9,8},{10,9},{11,1... | collective-permute-start | bytes 101384 | tf_op jit(solution)/shard_map/ppermute | solution.py:22
  64.5 1.3 collective-permute-start.17
  65.0 6.6 %collective-permute-start.20 = (f32[2,16,256]{2,1,0:T(8,128)S(1)}, f32[2,16,256]{2,1,0:T(8,128)S(1)}, u32[]{:S(2)}, u32[]{:S(2)}) collective-permute-start(f32[2,16,256]{2,1,0:T(8,128)S(1)} %get-tuple-element.34), channel_id=1, source_target_pairs={{0,16},{16,0},{1,17},{17,1},{2,18},{18,2},{3,19},{19,3},{4,20},{20... | collective-permute-start | bytes 98312 | tf_op jit(solution)/shard_map/ppermute | solution.py:20
  65.1 6.6 %collective-permute-start.21 = (f32[2,16,256]{2,1,0:T(8,128)S(1)}, f32[2,16,256]{2,1,0:T(8,128)S(1)}, u32[]{:S(2)}, u32[]{:S(2)}) collective-permute-start(f32[2,16,256]{2,1,0:T(8,128)S(1)} %get-tuple-element.35), channel_id=1, source_target_pairs={{16,0},{0,16},{17,1},{1,17},{18,2},{2,18},{19,3},{3,19},{20,4},{4,... | collective-permute-start | bytes 98312 | tf_op jit(solution)/shard_map/ppermute | solution.py:22
  65.8 11.5 %collective-permute-start.18 = (f32[20,2,128]{2,1,0:T(2,128)S(1)}, f32[20,2,128]{2,1,0:T(2,128)S(1)}, u32[]{:S(2)}, u32[]{:S(2)}) collective-permute-start(f32[20,2,128]{2,1,0:T(2,128)S(1)} %get-tuple-element.46), channel_id=1, source_target_pairs={{0,1},{1,2},{2,3},{3,4},{4,5},{5,6},{6,7},{7,8},{8,9},{9,10},{10,1... | collective-permute-start | bytes 61448 | tf_op jit(solution)/shard_map/ppermute | solution.py:20
  65.9 11.4 %collective-permute-start.19 = (f32[20,2,128]{2,1,0:T(2,128)S(1)}, f32[20,2,128]{2,1,0:T(2,128)S(1)}, u32[]{:S(2)}, u32[]{:S(2)}) collective-permute-start(f32[20,2,128]{2,1,0:T(2,128)S(1)} %get-tuple-element.47), channel_id=1, source_target_pairs={{1,0},{2,1},{3,2},{4,3},{5,4},{6,5},{7,6},{8,7},{9,8},{10,9},{11,1... | collective-permute-start | bytes 61448 | tf_op jit(solution)/shard_map/ppermute | solution.py:22
  71.7 7.7 %collective-permute-start.22 = (f32[20,2,256]{2,1,0:T(2,128)S(1)}, f32[20,2,256]{2,1,0:T(2,128)S(1)}, u32[]{:S(2)}, u32[]{:S(2)}) collective-permute-start(f32[20,2,256]{2,1,0:T(2,128)S(1)} %get-tuple-element.32), channel_id=1, source_target_pairs={{0,1},{1,2},{2,3},{3,4},{4,5},{5,6},{6,7},{7,8},{8,9},{9,10},{10,1... | collective-permute-start | bytes 122888 | tf_op jit(solution)/shard_map/ppermute | solution.py:20
  71.7 7.6 %collective-permute-start.23 = (f32[20,2,256]{2,1,0:T(2,128)S(1)}, f32[20,2,256]{2,1,0:T(2,128)S(1)}, u32[]{:S(2)}, u32[]{:S(2)}) collective-permute-start(f32[20,2,256]{2,1,0:T(2,128)S(1)} %get-tuple-element.33), channel_id=1, source_target_pairs={{1,0},{2,1},{3,2},{4,3},{5,4},{6,5},{7,6},{8,7},{9,8},{10,9},{11,1... | collective-permute-start | bytes 122888 | tf_op jit(solution)/shard_map/ppermute | solution.py:22
  79.6 1.2 collective-permute-start.24
  79.7 1.3 collective-permute-start.25
  81.0 7.4 %collective-permute-start.26 = (f32[20,2,128]{2,1,0:T(2,128)S(1)}, f32[20,2,128]{2,1,0:T(2,128)S(1)}, u32[]{:S(2)}, u32[]{:S(2)}) collective-permute-start(f32[20,2,128]{2,1,0:T(2,128)S(1)} %get-tuple-element.44), channel_id=1, source_target_pairs={{0,1},{1,2},{2,3},{3,4},{4,5},{5,6},{6,7},{7,8},{8,9},{9,10},{10,1... | collective-permute-start | bytes 61448 | tf_op jit(solution)/shard_map/ppermute | solution.py:20
  81.1 7.4 %collective-permute-start.27 = (f32[20,2,128]{2,1,0:T(2,128)S(1)}, f32[20,2,128]{2,1,0:T(2,128)S(1)}, u32[]{:S(2)}, u32[]{:S(2)}) collective-permute-start(f32[20,2,128]{2,1,0:T(2,128)S(1)} %get-tuple-element.45), channel_id=1, source_target_pairs={{1,0},{2,1},{3,2},{4,3},{5,4},{6,5},{7,6},{8,7},{9,8},{10,9},{11,1... | collective-permute-start | bytes 61448 | tf_op jit(solution)/shard_map/ppermute | solution.py:22
  88.8 1.2 collective-permute-start.28
  88.8 1.3 collective-permute-start.29
  90.2 7.5 %collective-permute-start.30 = (f32[20,2,128]{2,1,0:T(2,128)S(1)}, f32[20,2,128]{2,1,0:T(2,128)S(1)}, u32[]{:S(2)}, u32[]{:S(2)}) collective-permute-start(f32[20,2,128]{2,1,0:T(2,128)S(1)} %get-tuple-element.42), channel_id=1, source_target_pairs={{0,1},{1,2},{2,3},{3,4},{4,5},{5,6},{6,7},{7,8},{8,9},{9,10},{10,1... | collective-permute-start | bytes 61448 | tf_op jit(solution)/shard_map/ppermute | solution.py:20
  90.3 7.4 %collective-permute-start.31 = (f32[20,2,128]{2,1,0:T(2,128)S(1)}, f32[20,2,128]{2,1,0:T(2,128)S(1)}, u32[]{:S(2)}, u32[]{:S(2)}) collective-permute-start(f32[20,2,128]{2,1,0:T(2,128)S(1)} %get-tuple-element.43), channel_id=1, source_target_pairs={{1,0},{2,1},{3,2},{4,3},{5,4},{6,5},{7,6},{8,7},{9,8},{10,9},{11,1... | collective-permute-start | bytes 61448 | tf_op jit(solution)/shard_map/ppermute | solution.py:22
  98.0 1.3 collective-permute-start.33
  99.4 7.7 %collective-permute-start.34 = (f32[20,2,128]{2,1,0:T(2,128)S(1)}, f32[20,2,128]{2,1,0:T(2,128)S(1)}, u32[]{:S(2)}, u32[]{:S(2)}) collective-permute-start(f32[20,2,128]{2,1,0:T(2,128)S(1)} %get-tuple-element.40), channel_id=1, source_target_pairs={{0,1},{1,2},{2,3},{3,4},{4,5},{5,6},{6,7},{7,8},{8,9},{9,10},{10,1... | collective-permute-start | bytes 61448 | tf_op jit(solution)/shard_map/ppermute | solution.py:20
  99.5 7.6 %collective-permute-start.35 = (f32[20,2,128]{2,1,0:T(2,128)S(1)}, f32[20,2,128]{2,1,0:T(2,128)S(1)}, u32[]{:S(2)}, u32[]{:S(2)}) collective-permute-start(f32[20,2,128]{2,1,0:T(2,128)S(1)} %get-tuple-element.41), channel_id=1, source_target_pairs={{1,0},{2,1},{3,2},{4,3},{5,4},{6,5},{7,6},{8,7},{9,8},{10,9},{11,1... | collective-permute-start | bytes 61448 | tf_op jit(solution)/shard_map/ppermute | solution.py:22
  107.4 1.3 collective-permute-start.37
  108.8 7.5 %collective-permute-start.38 = (f32[20,2,128]{2,1,0:T(2,128)S(1)}, f32[20,2,128]{2,1,0:T(2,128)S(1)}, u32[]{:S(2)}, u32[]{:S(2)}) collective-permute-start(f32[20,2,128]{2,1,0:T(2,128)S(1)} %get-tuple-element.38), channel_id=1, source_target_pairs={{0,1},{1,2},{2,3},{3,4},{4,5},{5,6},{6,7},{7,8},{8,9},{9,10},{10,1... | collective-permute-start | bytes 61448 | tf_op jit(solution)/shard_map/ppermute | solution.py:20
  108.8 7.4 %collective-permute-start.39 = (f32[20,2,128]{2,1,0:T(2,128)S(1)}, f32[20,2,128]{2,1,0:T(2,128)S(1)}, u32[]{:S(2)}, u32[]{:S(2)}) collective-permute-start(f32[20,2,128]{2,1,0:T(2,128)S(1)} %get-tuple-element.39), channel_id=1, source_target_pairs={{1,0},{2,1},{3,2},{4,3},{5,4},{6,5},{7,6},{8,7},{9,8},{10,9},{11,1... | collective-permute-start | bytes 61448 | tf_op jit(solution)/shard_map/ppermute | solution.py:22
  116.6 1.3 collective-permute-start.41
  118.0 7.5 %collective-permute-start.42 = (f32[20,2,128]{2,1,0:T(2,128)S(1)}, f32[20,2,128]{2,1,0:T(2,128)S(1)}, u32[]{:S(2)}, u32[]{:S(2)}) collective-permute-start(f32[20,2,128]{2,1,0:T(2,128)S(1)} %get-tuple-element.36), channel_id=1, source_target_pairs={{0,1},{1,2},{2,3},{3,4},{4,5},{5,6},{6,7},{7,8},{8,9},{9,10},{10,1... | collective-permute-start | bytes 61448 | tf_op jit(solution)/shard_map/ppermute | solution.py:20
  118.1 7.4 %collective-permute-start.43 = (f32[20,2,128]{2,1,0:T(2,128)S(1)}, f32[20,2,128]{2,1,0:T(2,128)S(1)}, u32[]{:S(2)}, u32[]{:S(2)}) collective-permute-start(f32[20,2,128]{2,1,0:T(2,128)S(1)} %get-tuple-element.37), channel_id=1, source_target_pairs={{1,0},{2,1},{3,2},{4,3},{5,4},{6,5},{7,6},{8,7},{9,8},{10,9},{11,1... | collective-permute-start | bytes 61448 | tf_op jit(solution)/shard_map/ppermute | solution.py:22
  127.7 1.3 collective-permute-start.44
  127.8 1.4 collective-permute-start.45
  129.2 7.7 %collective-permute-start.46 = (f32[66,1,128]{2,1,0:T(1,128)S(1)}, f32[66,1,128]{2,1,0:T(1,128)S(1)}, u32[]{:S(2)}, u32[]{:S(2)}) collective-permute-start(f32[66,1,128]{2,1,0:T(1,128)S(1)} %get-tuple-element.10), channel_id=1, source_target_pairs={{0,1},{1,2},{2,3},{3,4},{4,5},{5,6},{6,7},{7,8},{8,9},{9,10},{10,1... | collective-permute-start | bytes 101384 | tf_op jit(solution)/shard_map/ppermute | solution.py:20
  129.2 7.6 %collective-permute-start.47 = (f32[66,1,128]{2,1,0:T(1,128)S(1)}, f32[66,1,128]{2,1,0:T(1,128)S(1)}, u32[]{:S(2)}, u32[]{:S(2)}) collective-permute-start(f32[66,1,128]{2,1,0:T(1,128)S(1)} %get-tuple-element.11), channel_id=1, source_target_pairs={{1,0},{2,1},{3,2},{4,3},{5,4},{6,5},{7,6},{8,7},{9,8},{10,9},{11,1... | collective-permute-start | bytes 101384 | tf_op jit(solution)/shard_map/ppermute | solution.py:22
  140.2 1.3 collective-permute-start.48
  140.3 1.4 collective-permute-start.49
  141.7 7.6 %collective-permute-start.50 = (f32[66,1,128]{2,1,0:T(1,128)S(1)}, f32[66,1,128]{2,1,0:T(1,128)S(1)}, u32[]{:S(2)}, u32[]{:S(2)}) collective-permute-start(f32[66,1,128]{2,1,0:T(1,128)S(1)} %get-tuple-element.8), channel_id=1, source_target_pairs={{0,1},{1,2},{2,3},{3,4},{4,5},{5,6},{6,7},{7,8},{8,9},{9,10},{10,1... | collective-permute-start | bytes 101384 | tf_op jit(solution)/shard_map/ppermute | solution.py:20
  141.8 7.6 %collective-permute-start.51 = (f32[66,1,128]{2,1,0:T(1,128)S(1)}, f32[66,1,128]{2,1,0:T(1,128)S(1)}, u32[]{:S(2)}, u32[]{:S(2)}) collective-permute-start(f32[66,1,128]{2,1,0:T(1,128)S(1)} %get-tuple-element.9), channel_id=1, source_target_pairs={{1,0},{2,1},{3,2},{4,3},{5,4},{6,5},{7,6},{8,7},{9,8},{10,9},{11,1... | collective-permute-start | bytes 101384 | tf_op jit(solution)/shard_map/ppermute | solution.py:22
  (9 other events, 39.0 us)
where the time goes:
time: 154 us
  starting transfers between devices  83.8 us (54%)
  other arithmetic  34.6 us (22%)
  waiting for transfers between devices  30.3 us (20%)
  local copies, waits for them, and re-layouts  4.38 us (3%)
    ppermute x26, starting transfers between devices, extended(): lax.ppermute(head, axis, [((i + 1) % count, i) for i in range(ends)])  78.5 us
    ppermute x26, waiting for transfers between devices, extended(): lax.ppermute(tail, axis, [(i, (i + 1) % count) for i in range(ends)])  28.5 us
    add x17, other arithmetic, smooth_step(): values + 0.8 * (load + cross_sum(padded) - (4.0 + mass_here) * values) /...  21.6 us
    sub x1, other arithmetic, shards(): load_terms + cross_sum(extended(values, (('band', 0), ('lane', 1)), 1, Tr...  9.06 us
    ppermute x26, starting transfers between devices, extended(): lax.ppermute(tail, axis, [(i, (i + 1) % count) for i in range(ends)])  5.36 us
  transfers between devices with their start and end apart: 52, of which 35 were waited for; matrix products, arithmetic and copies ran while one was open for 2% of the time, Pallas kernels for 0%

commit v1 on v0

v1 whole, which is shorter than its diff:
```python
import functools

import jax
import jax.numpy as jnp
from jax import lax
from jax.experimental import pallas as pl
from jax.experimental.pallas import tpu as pltpu
from jax.sharding import PartitionSpec as P

RATIO = 4
BEFORE = 3
AFTER = 2
INNER = 13
MESH = pl.DeviceIdType.MESH

PAD = 8
DEPTH = BEFORE + 1
ITEMS = DEPTH + 2 * (DEPTH - 1)
CPAD = 16


def kernel(lanes, bands, ny, nx, load_hbm, start_hbm, rate_hbm, out_hbm,
           ua, ub, fl, fw, ca, cb, c0, cw, tmp, stage,
           sx, rx, rc, csx, crx, crc, hsx, hrx, hry,
           in_sem, out_sem, xs, xr, ys, yr, cs, cr, kxs, kxr, kys, kyr, kcs, kcr, hxs, hxr, hys, hyr):
    lane, band = lax.axis_index("lane"), lax.axis_index("band")
    sides = ({"lane": lax.rem(lane + lanes - 1, lanes)}, {"lane": lax.rem(lane + 1, lanes)})
    ends = ({"band": lax.rem(band + bands - 1, bands)}, {"band": lax.rem(band + 1, bands)})
    ry, wx = ny + 2 * DEPTH, nx + 2 * PAD
    cy, cx = ny // RATIO, nx // RATIO
    cwx = cx + 2 * CPAD
    cry = cy + 2 * CPAD
    flat = lambda ref: ref.reshape(ref.shape[0] * ref.shape[1], ref.shape[2])
    fua, fub, ffl, ffw = flat(ua), flat(ub), flat(fl), flat(fw)
    fca, fcb, fc0, fcw = flat(ca), flat(cb), flat(c0), flat(cw)
    own = (pl.ds(DEPTH, ny), pl.ds(PAD, nx))

    ins = []
    for n, (src, dst) in enumerate(((start_hbm, ua), (load_hbm, fl), (rate_hbm, fw))):
        copy = pltpu.make_async_copy(src, dst.at[own[0], own[1]], in_sem.at[n])
        copy.start()
        ins.append(copy)

    barrier = pltpu.get_barrier_semaphore()
    for other in sides + ends:
        pl.semaphore_signal(barrier, inc=1, device_id=other, device_id_type=MESH)
    pl.semaphore_wait(barrier, 4)
    for copy in ins:
        copy.wait()

    def remote(src, dst, send, recv, other):
        copy = pltpu.make_async_remote_copy(src_ref=src, dst_ref=dst, send_sem=send, recv_sem=recv, device_id=other, device_id_type=MESH)
        copy.start()
        return copy

    arrays = [(fua, d) for d in range(DEPTH)] + [(ffl, d) for d in range(DEPTH - 1)] + [(ffw, d) for d in range(DEPTH - 1)]
    x_copies = []
    for side in range(2):
        for item, (ref, d) in enumerate(arrays):
            col = d if side == 0 else nx - 1 - d
            sx[side, item] = ref[pl.ds(DEPTH * wx + PAD + col, ny, stride=wx), :]
        x_copies.append(remote(sx.at[side], rx.at[1 - side], xs.at[side], xr.at[1 - side], sides[side]))

    y_copies = []
    for n, (ref, deep) in enumerate(((ua, DEPTH), (fl, DEPTH - 1), (fw, DEPTH - 1))):
        y_copies.append(remote(ref.at[pl.ds(DEPTH, deep), own[1]], ref.at[pl.ds(DEPTH + ny, deep), own[1]], ys.at[n, 0], yr.at[n, 1], ends[0]))
        y_copies.append(remote(ref.at[pl.ds(DEPTH + ny - deep, deep), own[1]], ref.at[pl.ds(DEPTH - deep, deep), own[1]], ys.at[n, 1], yr.at[n, 0], ends[1]))

    def blocks(rows_of, n):
        total = rows_of(0)
        for r in range(1, RATIO):
            total = total + rows_of(r)
        tmp[pl.ds(pl.multiple_of(n * wx, 8), nx), :] = total

    def across(n):
        base = n * wx
        total = tmp[pl.ds(base, cx, stride=RATIO), :]
        for j in range(1, RATIO):
            total = total + tmp[pl.ds(base + j, cx, stride=RATIO), :]
        return total * (1.0 / RATIO)

    def coarse_at(n):
        return pl.ds(pl.multiple_of((CPAD + n) * cwx + CPAD, 8), cx)

    def mass_row(n, carry):
        blocks(lambda r: ffw[pl.ds(pl.multiple_of((DEPTH + n * RATIO + r) * wx + PAD, 8), nx), :], n)
        fcw[coarse_at(n), :] = 0.8 / (4.0 + across(n))
        return carry

    lax.fori_loop(0, cy, mass_row, 0)

    def send_coarse(q, src):
        copies = []
        for side in range(2):
            for d in range(INNER):
                col = d if side == 0 else cx - 1 - d
                csx[side, q, d] = src[pl.ds(CPAD * cwx + CPAD + col, cy, stride=cwx), :]
            copies.append(remote(csx.at[side, q], crx.at[1 - side, q], kxs.at[side, q], kxr.at[1 - side, q], sides[side]))
        return copies

    def send_rows(q, ref):
        mine = ref.at[pl.ds(CPAD, cy), pl.ds(CPAD, cx)]
        return [
            remote(mine, ref.at[pl.ds(CPAD + cy, cy), pl.ds(CPAD, cx)], kys.at[0, q], kyr.at[1, q], ends[0]),
            remote(mine, ref.at[pl.ds(CPAD - cy, cy), pl.ds(CPAD, cx)], kys.at[1, q], kyr.at[0, q], ends[1]),
        ]

    def forward(q, side):
        return [remote(crx.at[side, q], crc.at[side, q, 1 - end], kcs.at[side, q, end], kcr.at[side, q, 1 - end], ends[end]) for end in range(2)]

    def unpack_coarse(q, dst):
        for side in range(2):
            for d in range(INNER):
                col = CPAD - 1 - d if side == 0 else CPAD + cx + d
                dst[pl.ds(CPAD * cwx + col, cy, stride=cwx), :] = crx[side, q, d]
                dst[pl.ds((CPAD - cy) * cwx + col, cy, stride=cwx), :] = crc[side, q, 0, d]
                dst[pl.ds((CPAD + cy) * cwx + col, cy, stride=cwx), :] = crc[side, q, 1, d]

    mass_x = send_coarse(0, fcw)
    mass_y = send_rows(0, cw)

    c_copies = []
    for side in range(2):
        x_copies[1 - side].wait_recv()
        for end in range(2):
            rows = pl.ds(0, 8) if end == 0 else pl.ds(ny - 8, 8)
            c_copies.append(remote(rx.at[side, :, rows], rc.at[side, 1 - end], cs.at[side, end], cr.at[side, 1 - end], ends[end]))
    for copy in y_copies:
        copy.wait()
    for side in range(2):
        for item, (ref, d) in enumerate(arrays):
            col = PAD - 1 - d if side == 0 else PAD + nx + d
            ref[pl.ds(DEPTH * wx + col, ny, stride=wx), :] = rx[side, item]
    for copy in c_copies:
        copy.wait()
    for side in range(2):
        for item, (ref, d) in enumerate(arrays):
            col = PAD - 1 - d if side == 0 else PAD + nx + d
            ref[pl.ds(col, DEPTH, stride=wx), :] = rc[side, 0, item, 8 - DEPTH:8]
            ref[pl.ds((DEPTH + ny) * wx + col, DEPTH, stride=wx), :] = rc[side, 1, item, 0:DEPTH]

    def weigh(y, carry):
        at = pl.ds(pl.multiple_of(y * wx, 8), wx)
        weight = 0.8 / (4.0 + ffw[at, :])
        ffw[at, :] = weight
        ffl[at, :] = weight * ffl[at, :]
        return carry

    lax.fori_loop(0, ry, weigh, 0)

    def sweep(src, dst, load, weight, width, first, count, low, high, put=None):
        def rows(n, carry):
            for r in range(2):
                y = first + 2 * n + r
                base = pl.multiple_of(y * width + low, 8)
                span = high - low
                here = src[pl.ds(base, span), :]
                around = (src[pl.ds(base - width, span), :] + src[pl.ds(base + width, span), :]
                          + src[pl.ds(base - 1, span), :] + src[pl.ds(base + 1, span), :])
                new = 0.2 * here + weight[pl.ds(base, span), :] * around + load[pl.ds(base, span), :]
                if put is None:
                    dst[pl.ds(base, span), :] = new
                else:
                    put(y, new)
            return carry

        lax.fori_loop(0, count // 2, rows, 0)

    sweep(fua, fub, ffl, ffw, wx, 1, ry - 2, 0, wx)
    sweep(fub, fua, ffl, ffw, wx, 2, ry - 4, 0, wx)
    sweep(fua, fub, ffl, ffw, wx, 3, ry - 6, 0, wx)

    h_copies = []
    for side in range(2):
        col = 1 if side == 0 else nx - 2
        hsx[side] = fub[pl.ds(DEPTH * wx + PAD + col, ny, stride=wx), :]
        h_copies.append(remote(hsx.at[side], hrx.at[1 - side], hxs.at[side], hxr.at[1 - side], sides[side]))
    hy_copies = [
        remote(ub.at[DEPTH + 1, own[1]], hry.at[1], hys.at[0], hyr.at[1], ends[0]),
        remote(ub.at[DEPTH + ny - 2, own[1]], hry.at[0], hys.at[1], hyr.at[0], ends[1]),
    ]

    def load_row(n, carry):
        def defect(r):
            base = pl.multiple_of((DEPTH + n * RATIO + r) * wx + PAD, 8)
            weight = ffw[pl.ds(base, nx), :]
            around = (fub[pl.ds(base - wx, nx), :] + fub[pl.ds(base + wx, nx), :]
                      + fub[pl.ds(base - 1, nx), :] + fub[pl.ds(base + 1, nx), :])
            return around + (ffl[pl.ds(base, nx), :] - 0.8 * fub[pl.ds(base, nx), :]) / weight

        blocks(defect, n)
        fc0[coarse_at(n), :] = fcw[coarse_at(n), :] * across(n)
        return carry

    lax.fori_loop(0, cy, load_row, 0)

    load_x = send_coarse(1, fc0)
    load_y = send_rows(1, c0)
    forwards = []
    for side in range(2):
        mass_x[1 - side].wait_recv()
        forwards += forward(0, side)
    for copy in mass_y + forwards:
        copy.wait()
    unpack_coarse(0, fcw)
    forwards = []
    for side in range(2):
        load_x[1 - side].wait_recv()
        forwards += forward(1, side)
    for copy in load_y + forwards:
        copy.wait()
    unpack_coarse(1, fc0)

    now, later = fc0, fca
    for t in range(2, INNER + 1):
        reach = INNER + 1 - t
        low = (CPAD - reach) // 8 * 8
        high = -((-(CPAD + cx + reach)) // 8) * 8
        sweep(now, later, fc0, fcw, cwx, CPAD - reach, cy + 2 * reach, low, high)
        now, later = later, (fcb if t % 2 == 0 else fca)

    for copy in h_copies:
        copy.wait_recv()
    for copy in hy_copies:
        copy.wait()
    for side in range(2):
        col = PAD - 2 if side == 0 else PAD + nx + 1
        fub[pl.ds(DEPTH * wx + col, ny, stride=wx), :] = hrx[side]
    ub[DEPTH - 2, own[1]] = hry[0]
    ub[DEPTH + ny + 1, own[1]] = hry[1]
    count = wx // RATIO
    for n in range(cy + 2):
        row = now[pl.ds((CPAD - 1 + n) * cwx + CPAD - PAD // RATIO, count), :]
        for j in range(RATIO):
            tmp[pl.ds(n * wx + j, count, stride=RATIO), :] = row

    def correct(n, carry):
        extra = tmp[pl.ds(pl.multiple_of(n * wx, 8), wx), :]
        for r in range(RATIO):
            at = pl.ds(pl.multiple_of((n * RATIO + r) * wx, 8), wx)
            fub[at, :] = fub[at, :] + extra
        return carry

    lax.fori_loop(0, cy + 2, correct, 0)
    sweep(fub, fua, ffl, ffw, wx, DEPTH - 1, ny + 2, 0, wx)

    def put(y, new):
        stage[y - DEPTH] = new

    pieces = 4
    outs = []
    for piece in range(pieces):
        part = ny // pieces
        sweep(fua, None, ffl, ffw, wx, DEPTH + piece * part, part, PAD, PAD + nx, put)
        at = pl.ds(piece * part, part)
        copy = pltpu.make_async_copy(stage.at[at], out_hbm.at[at], out_sem.at[piece])
        copy.start()
        outs.append(copy)
    for copy in x_copies + mass_x + load_x + h_copies:
        copy.wait_send()
    for copy in outs:
        copy.wait()


def shards(lanes, bands, load_terms, start_values, reaction_rate):
    ny, nx, layers = load_terms.shape
    f32 = jnp.float32
    ry, wx = ny + 2 * DEPTH, nx + 2 * PAD
    cy, cx = ny // RATIO, nx // RATIO
    assert ny % 8 == 0 and nx % 8 == 0 and INNER <= min(cy, cx) <= CPAD and layers == 128
    fine = pltpu.VMEM((ry, wx, layers), f32)
    coarse = pltpu.VMEM((cy + 2 * CPAD, cx + 2 * CPAD, layers), f32)
    dma = pltpu.SemaphoreType.DMA
    return pl.pallas_call(
        functools.partial(kernel, lanes, bands, ny, nx),
        out_shape=jax.ShapeDtypeStruct(load_terms.shape, f32),
        in_specs=[pl.BlockSpec(memory_space=pl.ANY)] * 3,
        out_specs=pl.BlockSpec(memory_space=pl.ANY),
        scratch_shapes=[
            fine, fine, fine, fine, coarse, coarse, coarse, coarse,
            pltpu.VMEM(((cy + 2) * wx, layers), f32),
            pltpu.VMEM((ny, nx, layers), f32),
            pltpu.VMEM((2, ITEMS, ny, layers), f32),
            pltpu.VMEM((2, ITEMS, ny, layers), f32),
            pltpu.VMEM((2, 2, ITEMS, 8, layers), f32),
            pltpu.VMEM((2, 2, INNER, cy, layers), f32),
            pltpu.VMEM((2, 2, INNER, cy, layers), f32),
            pltpu.VMEM((2, 2, 2, INNER, cy, layers), f32),
            pltpu.VMEM((2, ny, layers), f32),
            pltpu.VMEM((2, ny, layers), f32),
            pltpu.VMEM((2, nx, layers), f32),
            dma((3,)), dma((4,)),
            dma((2,)), dma((2,)), dma((3, 2)), dma((3, 2)), dma((2, 2)), dma((2, 2)),
            dma((2, 2)), dma((2, 2)), dma((2, 2)), dma((2, 2)), dma((2, 2, 2)), dma((2, 2, 2)),
            dma((2,)), dma((2,)), dma((2,)), dma((2,)),
        ],
        compiler_params=pltpu.CompilerParams(collective_id=0, has_side_effects=True, vmem_limit_bytes=60 * 2**20),
    )(load_terms, start_values, reaction_rate)


def solution(mesh):
    spec = P("band", "lane", None)
    return jax.shard_map(
        functools.partial(shards, mesh.shape["lane"], mesh.shape["band"]),
        mesh=mesh,
        in_specs=(spec, spec, spec),
        out_specs=spec,
        check_vma=False,
    )
```

time: 154 us -> 50 us (0.32)
  the two profiles are of different devices: /device:TPU:0 before, /device:TPU:5 now
where the time goes in v1:
time: 50 us; the launch traced here: 49.6 us
  Pallas kernels  46.5 us (93%)
  local copies, waits for them, and re-layouts  3.16 us (6%)
    pallas_call x1, Pallas kernels, shards(): pl.pallas_call(functools.partial(kernel, lanes, bands, ny, nx), out_shape...  46.5 us
    unnamed x1, local copies, waits for them, and re-layouts  3.16 us

profile of v1, /device:TPU:5, one launch (start us, length us, event | category | flops | bytes accessed | tf_op | source)
XLA Modules:
  0.0 49.6 jit_solution(15892826165117855368)
XLA Ops:
  0.0 46.5 %shard_map.37 = f32[64,64,128]{2,1,0:T(8,128)} custom-call(f32[64,64,128]{2,1,0:T(8,128)} %load_hbm.1, f32[64,64,128]{2,1,0:T(8,128)} %start_hbm.1, f32[64,64,128]{2,1,0:T(8,128)} %rate_hbm.1), custom_call_target="tpu_custom_call" | custom-call | tf_op jit(solution)/shard_map/pallas_call | solution.py:274
  46.5 3.2 %copy.5 = f32[64,64,128]{2,1,0:T(8,128)} copy(f32[64,64,128]{2,1,0:T(8,128)} %shard_map.37) | data formatting | bytes 4194304

commit v2 on v1

v2 whole, which is shorter than its diff:
```python
import functools

import jax
import jax.numpy as jnp
from jax import lax
from jax.experimental import pallas as pl
from jax.experimental.pallas import tpu as pltpu
from jax.sharding import PartitionSpec as P

RATIO = 4
BEFORE = 3
AFTER = 2
INNER = 13
MESH = pl.DeviceIdType.MESH

PAD = 8
DEPTH = BEFORE + 1
ITEMS = BEFORE + 3
CPAD = 16


def kernel(lanes, bands, ny, nx, load_hbm, start_hbm, rate_hbm, out_hbm,
           u0, u1, u2, u3, fl, fw, ca, cb, c0, cw, tmp, stage,
           sx, rx, line, held, csx, crx, crc, hsx, hrx, hry,
           in_sem, out_sem, xs, xr, ys, yr, kxs, kxr, kys, kyr, kcs, kcr, hxs, hxr, hys, hyr):
    lane, band = lax.axis_index("lane"), lax.axis_index("band")
    sides = ({"lane": lax.rem(lane + lanes - 1, lanes)}, {"lane": lax.rem(lane + 1, lanes)})
    ends = ({"band": lax.rem(band + bands - 1, bands)}, {"band": lax.rem(band + 1, bands)})
    ry, wx = ny + 2 * DEPTH, nx + 2 * PAD
    cy, cx = ny // RATIO, nx // RATIO
    cwx = cx + 2 * CPAD
    flat = lambda ref: ref.reshape(ref.shape[0] * ref.shape[1], ref.shape[2])
    fu0, fu1, fu2, fu3, ffl, ffw = flat(u0), flat(u1), flat(u2), flat(u3), flat(fl), flat(fw)
    fca, fcb, fc0, fcw = flat(ca), flat(cb), flat(c0), flat(cw)
    own = (pl.ds(DEPTH, ny), pl.ds(PAD, nx))

    cols = (pl.ds(PAD, 8), pl.ds(PAD + nx - 8, 8), pl.ds(PAD + 8, nx - 16))
    takes = (pl.ds(0, 8), pl.ds(nx - 8, 8), pl.ds(8, nx - 16))
    ins = []
    for part in range(3):
        for n, (src, dst) in enumerate(((start_hbm, u0), (load_hbm, fl), (rate_hbm, fw))):
            copy = pltpu.make_async_copy(src.at[:, takes[part]], dst.at[own[0], cols[part]], in_sem.at[n, part])
            copy.start()
            ins.append(copy)

    barrier = pltpu.get_barrier_semaphore()
    for other in sides + ends:
        pl.semaphore_signal(barrier, inc=1, device_id=other, device_id_type=MESH)
    pl.semaphore_wait(barrier, 4)

    def remote(src, dst, send, recv, other):
        copy = pltpu.make_async_remote_copy(src_ref=src, dst_ref=dst, send_sem=send, recv_sem=recv, device_id=other, device_id_type=MESH)
        copy.start()
        return copy

    def send_edges(part):
        copies = []
        for n, (ref, deep) in enumerate(((u0, DEPTH), (fl, DEPTH - 1), (fw, DEPTH - 1))):
            copies.append(remote(ref.at[pl.ds(DEPTH, deep), cols[part]], ref.at[pl.ds(DEPTH + ny, deep), cols[part]], ys.at[n, part, 0], yr.at[n, part, 1], ends[0]))
            copies.append(remote(ref.at[pl.ds(DEPTH + ny - deep, deep), cols[part]], ref.at[pl.ds(DEPTH - deep, deep), cols[part]], ys.at[n, part, 1], yr.at[n, part, 0], ends[1]))
        return copies

    for copy in ins[:6]:
        copy.wait()
    edge_copies = send_edges(0) + send_edges(1)

    def column(ref, col, first=0, count=ry):
        return ref[pl.ds(first * wx + col, count, stride=wx), :]

    for ref in (fu0, fu1, fu2):
        for col in (PAD - 1, PAD + nx):
            ref[pl.ds(col, ry, stride=wx), :] = jnp.zeros((ry, ref.shape[1]), jnp.float32)
    for copy in edge_copies:
        copy.wait()

    inner = pl.ds(8, ry)

    def about(ref):
        return ref[pl.ds(7, ry), :] + ref[pl.ds(9, ry), :]

    x_copies = []
    kept = []
    for side in range(2):
        where = [PAD + d if side == 0 else PAD + nx - 1 - d for d in range(DEPTH)]
        values = [column(fu0, col) for col in where]
        weights = [0.8 / (4.0 + column(ffw, col)) for col in where[:3]]
        loads = [weight * column(ffl, col) for weight, col in zip(weights, where)]
        sx[side, 0] = values[0]
        sx[side, 1] = weights[0]
        sx[side, 2] = weights[0] * weights[0] * weights[1]
        sx[side, 3] = weights[0] * values[1] + loads[0]
        x_copies.append(remote(sx.at[side, pl.ds(0, 4)], rx.at[1 - side, pl.ds(0, 4)], xs.at[side, 0], xr.at[1 - side, 0], sides[side]))
        for d in range(3):
            line[d, inner] = values[d]
        once = []
        for d in range(3):
            around = about(line.at[d]) + values[d + 1]
            if d > 0:
                around = around + values[d - 1]
            once.append(0.2 * values[d] + weights[d] * around + loads[d])
        sx[side, 4] = weights[0] * once[1] + loads[0]
        line[3, inner] = once[1]
        twice = 0.2 * once[1] + weights[1] * (about(line.at[3]) + once[0] + once[2]) + loads[1]
        sx[side, 5] = weights[0] * twice + loads[0]
        x_copies.append(remote(sx.at[side, pl.ds(4, 2)], rx.at[1 - side, pl.ds(4, 2)], xs.at[side, 1], xr.at[1 - side, 1], sides[side]))

    for copy in ins[6:]:
        copy.wait()
    mid_copies = send_edges(2)

    def blocks(rows_of, n):
        total = rows_of(0)
        for r in range(1, RATIO):
            total = total + rows_of(r)
        tmp[pl.ds(pl.multiple_of(n * wx, 8), nx), :] = total

    def across(n):
        base = n * wx
        total = tmp[pl.ds(base, cx, stride=RATIO), :]
        for j in range(1, RATIO):
            total = total + tmp[pl.ds(base + j, cx, stride=RATIO), :]
        return total * (1.0 / RATIO)

    def coarse_at(n):
        return pl.ds(pl.multiple_of((CPAD + n) * cwx + CPAD, 8), cx)

    def mass_row(n, carry):
        blocks(lambda r: ffw[pl.ds(pl.multiple_of((DEPTH + n * RATIO + r) * wx + PAD, 8), nx), :], n)
        fcw[coarse_at(n), :] = 0.8 / (4.0 + across(n))
        return carry

    lax.fori_loop(0, cy, mass_row, 0)

    def send_coarse(q, src):
        copies = []
        for side in range(2):
            for d in range(INNER):
                col = d if side == 0 else cx - 1 - d
                csx[side, q, d] = src[pl.ds(CPAD * cwx + CPAD + col, cy, stride=cwx), :]
            copies.append(remote(csx.at[side, q], crx.at[1 - side, q], kxs.at[side, q], kxr.at[1 - side, q], sides[side]))
        return copies

    def send_rows(q, ref):
        mine = ref.at[pl.ds(CPAD, cy), pl.ds(CPAD, cx)]
        return [
            remote(mine, ref.at[pl.ds(CPAD + cy, cy), pl.ds(CPAD, cx)], kys.at[0, q], kyr.at[1, q], ends[0]),
            remote(mine, ref.at[pl.ds(CPAD - cy, cy), pl.ds(CPAD, cx)], kys.at[1, q], kyr.at[0, q], ends[1]),
        ]

    def forward(q, side):
        return [remote(crx.at[side, q], crc.at[side, q, 1 - end], kcs.at[side, q, end], kcr.at[side, q, 1 - end], ends[end]) for end in range(2)]

    def unpack_coarse(q, dst):
        for side in range(2):
            for d in range(INNER):
                col = CPAD - 1 - d if side == 0 else CPAD + cx + d
                dst[pl.ds(CPAD * cwx + col, cy, stride=cwx), :] = crx[side, q, d]
                dst[pl.ds((CPAD - cy) * cwx + col, cy, stride=cwx), :] = crc[side, q, 0, d]
                dst[pl.ds((CPAD + cy) * cwx + col, cy, stride=cwx), :] = crc[side, q, 1, d]

    mass_x = send_coarse(0, fcw)
    mass_y = send_rows(0, cw)

    for copy in mid_copies:
        copy.wait()

    def weigh(y, carry):
        at = pl.ds(pl.multiple_of(y * wx + PAD, 8), nx)
        weight = 0.8 / (4.0 + ffw[at, :])
        ffw[at, :] = weight
        ffl[at, :] = weight * ffl[at, :]
        return carry

    lax.fori_loop(0, ry, weigh, 0)

    def sweep(src, dst, load, weight, width, first, count, ranges, put=None, group=2):
        def rows(n, carry):
            for r in range(group):
                for low, high in ranges:
                    y = first + group * n + r
                    base = pl.multiple_of(y * width + low, 8)
                    span = high - low
                    here = src[pl.ds(base, span), :]
                    around = (src[pl.ds(base - width, span), :] + src[pl.ds(base + width, span), :]
                              + src[pl.ds(base - 1, span), :] + src[pl.ds(base + 1, span), :])
                    new = 0.2 * here + weight[pl.ds(base, span), :] * around + load[pl.ds(base, span), :]
                    if put is None:
                        dst[pl.ds(base, span), :] = new
                    else:
                        put(y, new)
            return carry

        lax.fori_loop(0, count // group, rows, 0)

    def defect_rows(low, span):
        def row(n, carry):
            total = None
            for r in range(RATIO):
                base = pl.multiple_of((DEPTH + n * RATIO + r) * wx + low, 8)
                around = (fu3[pl.ds(base - wx, span), :] + fu3[pl.ds(base + wx, span), :]
                          + fu3[pl.ds(base - 1, span), :] + fu3[pl.ds(base + 1, span), :])
                here = around + (ffl[pl.ds(base, span), :] - 0.8 * fu3[pl.ds(base, span), :]) / ffw[pl.ds(base, span), :]
                total = here if total is None else total + here
            tmp[pl.ds(pl.multiple_of(n * wx + low - PAD, 8), span), :] = total
            return carry

        lax.fori_loop(0, cy, row, 0)

    whole = ((PAD, PAD + nx),)
    sweep(fu0, fu1, ffl, ffw, wx, 1, ry - 2, whole)
    sweep(fu1, fu2, ffl, ffw, wx, 2, ry - 4, whole)
    sweep(fu2, fu3, ffl, ffw, wx, 3, ry - 6, whole)
    defect_rows(PAD + 8, nx - 16)

    for copy in x_copies:
        copy.wait_recv()
    edges = ((PAD, PAD + 8), (PAD + nx - 8, PAD + nx))
    lanes_of = ((PAD - 1, PAD), (PAD + nx, PAD + nx - 1))
    fine = (fu0, fu1, fu2, fu3)
    for t in range(BEFORE):
        for side, (halo, near) in enumerate(lanes_of):
            if t == 0:
                held[side, 0, inner] = rx[side, 0]
            here = held[side, t, inner]
            fine[t][pl.ds(halo, ry, stride=wx), :] = here
            new = 0.2 * here + rx[side, 1] * (about(held.at[side, t]) + column(fine[t], near)) + rx[side, 3 + t]
            if t == 2:
                new = new + rx[side, 2] * column(fu0, near)
            held[side, t + 1, inner] = new
        sweep(fine[t], fine[t + 1], ffl, ffw, wx, 1, ry - 2, edges, None, 10 if (ry - 2) % 10 == 0 else 2)
    for side, (halo, near) in enumerate(lanes_of):
        fu3[pl.ds(halo, ry, stride=wx), :] = held[side, BEFORE, inner]
    for low, high in edges:
        defect_rows(low, high - low)

    h_copies = []

    def load_row(n, carry):
        fc0[coarse_at(n), :] = fcw[coarse_at(n), :] * across(n)
        return carry

    lax.fori_loop(0, cy, load_row, 0)

    load_x = send_coarse(1, fc0)
    load_y = send_rows(1, c0)
    for side in range(2):
        col, second = (PAD, PAD + 1) if side == 0 else (PAD + nx - 1, PAD + nx - 2)
        hsx[side] = column(ffw, col, DEPTH, ny) * column(fu3, second, DEPTH, ny) + column(ffl, col, DEPTH, ny)
        h_copies.append(remote(hsx.at[side], hrx.at[1 - side], hxs.at[side], hxr.at[1 - side], sides[side]))
    hy_copies = [
        remote(u3.at[DEPTH + 1, own[1]], hry.at[1], hys.at[0], hyr.at[1], ends[0]),
        remote(u3.at[DEPTH + ny - 2, own[1]], hry.at[0], hys.at[1], hyr.at[0], ends[1]),
    ]
    forwards = []
    for side in range(2):
        mass_x[1 - side].wait_recv()
        forwards += forward(0, side)
    for copy in mass_y + forwards:
        copy.wait()
    unpack_coarse(0, fcw)
    forwards = []
    for side in range(2):
        load_x[1 - side].wait_recv()
        forwards += forward(1, side)
    for copy in load_y + forwards:
        copy.wait()
    unpack_coarse(1, fc0)

    now, later = fc0, fca
    for t in range(2, INNER + 1):
        reach = INNER + 1 - t
        low = (CPAD - reach) // 8 * 8
        high = -((-(CPAD + cx + reach)) // 8) * 8
        sweep(now, later, fc0, fcw, cwx, CPAD - reach, cy + 2 * reach, ((low, high),))
        now, later = later, (fcb if t % 2 == 0 else fca)

    for copy in h_copies:
        copy.wait_recv()
    for copy in hy_copies:
        copy.wait()
    u3[DEPTH - 2, own[1]] = hry[0]
    u3[DEPTH + ny + 1, own[1]] = hry[1]
    count = wx // RATIO
    for n in range(cy + 2):
        row = now[pl.ds((CPAD - 1 + n) * cwx + CPAD - PAD // RATIO, count), :]
        for j in range(RATIO):
            tmp[pl.ds(n * wx + j, count, stride=RATIO), :] = row

    def correct(n, carry):
        extra = tmp[pl.ds(pl.multiple_of(n * wx, 8), wx), :]
        for r in range(RATIO):
            at = pl.ds(pl.multiple_of((n * RATIO + r) * wx, 8), wx)
            fu3[at, :] = fu3[at, :] + extra
        return carry

    lax.fori_loop(0, cy + 2, correct, 0)
    sweep(fu3, fu0, ffl, ffw, wx, DEPTH - 1, ny + 2, whole)
    for side, (halo, near) in enumerate(lanes_of):
        here = column(fu3, halo, DEPTH, ny)
        change = here - held[side, BEFORE, pl.ds(8 + DEPTH, ny)]
        around = column(fu3, halo, DEPTH - 1, ny) + column(fu3, halo, DEPTH + 1, ny) + column(fu3, near, DEPTH, ny) + change
        fu0[pl.ds(DEPTH * wx + halo, ny, stride=wx), :] = 0.2 * here + rx[side, 1, pl.ds(DEPTH, ny)] * around + hrx[side]

    def put(y, new):
        stage[y - DEPTH] = new

    pieces = 4
    outs = []
    for piece in range(pieces):
        part = ny // pieces
        sweep(fu0, None, ffl, ffw, wx, DEPTH + piece * part, part, whole, put)
        at = pl.ds(piece * part, part)
        copy = pltpu.make_async_copy(stage.at[at], out_hbm.at[at], out_sem.at[piece])
        copy.start()
        outs.append(copy)
    for copy in x_copies + mass_x + load_x + h_copies:
        copy.wait_send()
    for copy in outs:
        copy.wait()


def shards(lanes, bands, load_terms, start_values, reaction_rate):
    ny, nx, layers = load_terms.shape
    f32 = jnp.float32
    ry, wx = ny + 2 * DEPTH, nx + 2 * PAD
    cy, cx = ny // RATIO, nx // RATIO
    assert ny % 8 == 0 and nx % 8 == 0 and INNER <= min(cy, cx) <= CPAD and layers == 128
    fine = pltpu.VMEM((ry, wx, layers), f32)
    coarse = pltpu.VMEM((cy + 2 * CPAD, cx + 2 * CPAD, layers), f32)
    dma = pltpu.SemaphoreType.DMA
    return pl.pallas_call(
        functools.partial(kernel, lanes, bands, ny, nx),
        out_shape=jax.ShapeDtypeStruct(load_terms.shape, f32),
        in_specs=[pl.BlockSpec(memory_space=pl.ANY)] * 3,
        out_specs=pl.BlockSpec(memory_space=pl.ANY),
        scratch_shapes=[
            fine, fine, fine, fine, fine, fine, coarse, coarse, coarse, coarse,
            pltpu.VMEM(((cy + 2) * wx, layers), f32),
            pltpu.VMEM((ny, nx, layers), f32),
            pltpu.VMEM((2, ITEMS, ry, layers), f32),
            pltpu.VMEM((2, ITEMS, ry, layers), f32),
            pltpu.VMEM((4, ry + 16, layers), f32),
            pltpu.VMEM((2, DEPTH, ry + 16, layers), f32),
            pltpu.VMEM((2, 2, INNER, cy, layers), f32),
            pltpu.VMEM((2, 2, INNER, cy, layers), f32),
            pltpu.VMEM((2, 2, 2, INNER, cy, layers), f32),
            pltpu.VMEM((2, ny, layers), f32),
            pltpu.VMEM((2, ny, layers), f32),
            pltpu.VMEM((2, nx, layers), f32),
            dma((3, 3)), dma((4,)),
            dma((2, 2)), dma((2, 2)), dma((3, 3, 2)), dma((3, 3, 2)),
            dma((2, 2)), dma((2, 2)), dma((2, 2)), dma((2, 2)), dma((2, 2, 2)), dma((2, 2, 2)),
            dma((2,)), dma((2,)), dma((2,)), dma((2,)),
        ],
        compiler_params=pltpu.CompilerParams(collective_id=0, has_side_effects=True, vmem_limit_bytes=60 * 2**20),
    )(load_terms, start_values, reaction_rate)


def solution(mesh):
    spec = P("band", "lane", None)
    return jax.shard_map(
        functools.partial(shards, mesh.shape["lane"], mesh.shape["band"]),
        mesh=mesh,
        in_specs=(spec, spec, spec),
        out_specs=spec,
        check_vma=False,
    )
```

time: 50 us -> 43.6 us (0.87)
  Pallas kernels: 46.5 us -> 40.3 us
    pallas_call x1, Pallas kernels: 46.5 us -> 40.3 us  [shards(): pl.pallas_call(functools.partial(kernel, lanes, bands, ny, nx), out_shape...]
where the time goes in v2:
time: 43.6 us; the launch traced here: 43.5 us
  Pallas kernels  40.3 us (92%)
  local copies, waits for them, and re-layouts  3.16 us (7%)
    pallas_call x1, Pallas kernels, shards(): pl.pallas_call(functools.partial(kernel, lanes, bands, ny, nx), out_shape...  40.3 us
    unnamed x1, local copies, waits for them, and re-layouts  3.16 us

profile of v2, /device:TPU:5, one launch (start us, length us, event | category | flops | bytes accessed | tf_op | source)
XLA Modules:
  0.0 43.5 jit_solution(1111987599638894589)
XLA Ops:
  0.0 40.3 %shard_map.37 = f32[64,64,128]{2,1,0:T(8,128)} custom-call(f32[64,64,128]{2,1,0:T(8,128)} %load_hbm.1, f32[64,64,128]{2,1,0:T(8,128)} %start_hbm.1, f32[64,64,128]{2,1,0:T(8,128)} %rate_hbm.1), custom_call_target="tpu_custom_call" | custom-call | tf_op jit(solution)/shard_map/pallas_call | solution.py:331
  40.3 3.2 %copy.5 = f32[64,64,128]{2,1,0:T(8,128)} copy(f32[64,64,128]{2,1,0:T(8,128)} %shard_map.37) | data formatting | bytes 4194304

commit v3 on v2

--- a/solution.py
+++ b/solution.py
@@ -175,42 +175,48 @@
 
     def sweep(src, dst, load, weight, width, first, count, ranges, put=None, group=2):
         def rows(n, carry):
-            for r in range(group):
-                for low, high in ranges:
-                    y = first + group * n + r
-                    base = pl.multiple_of(y * width + low, 8)
-                    span = high - low
-                    here = src[pl.ds(base, span), :]
-                    around = (src[pl.ds(base - width, span), :] + src[pl.ds(base + width, span), :]
-                              + src[pl.ds(base - 1, span), :] + src[pl.ds(base + 1, span), :])
-                    new = 0.2 * here + weight[pl.ds(base, span), :] * around + load[pl.ds(base, span), :]
+            for low, high in ranges:
+                span = high - low
+                base = pl.multiple_of((first + group * n) * width + low, 8)
+                above, here = src[pl.ds(base - width, span), :], src[pl.ds(base, span), :]
+                for r in range(group):
+                    at = base + r * width
+                    below = src[pl.ds(at + width, span), :]
+                    around = (above + below) + (src[pl.ds(at - 1, span), :] + src[pl.ds(at + 1, span), :])
+                    new = 0.2 * here + weight[pl.ds(at, span), :] * around + load[pl.ds(at, span), :]
                     if put is None:
-                        dst[pl.ds(base, span), :] = new
+                        dst[pl.ds(at, span), :] = new
                     else:
-                        put(y, new)
+                        put(first + group * n + r, new)
+                    above, here = here, below
             return carry
 
-        lax.fori_loop(0, count // group, rows, 0)
-
-    def defect_rows(low, span):
+        lax.fori_loop(0, -(-count // group), rows, 0)
+
+    def defect_rows(ranges):
         def row(n, carry):
-            total = None
-            for r in range(RATIO):
-                base = pl.multiple_of((DEPTH + n * RATIO + r) * wx + low, 8)
-                around = (fu3[pl.ds(base - wx, span), :] + fu3[pl.ds(base + wx, span), :]
-                          + fu3[pl.ds(base - 1, span), :] + fu3[pl.ds(base + 1, span), :])
-                here = around + (ffl[pl.ds(base, span), :] - 0.8 * fu3[pl.ds(base, span), :]) / ffw[pl.ds(base, span), :]
-                total = here if total is None else total + here
-            tmp[pl.ds(pl.multiple_of(n * wx + low - PAD, 8), span), :] = total
+            for low, high in ranges:
+                span = high - low
+                base = pl.multiple_of((DEPTH + n * RATIO) * wx + low, 8)
+                above, here = fu3[pl.ds(base - wx, span), :], fu3[pl.ds(base, span), :]
+                total = None
+                for r in range(RATIO):
+                    at = base + r * wx
+                    below = fu3[pl.ds(at + wx, span), :]
+                    around = (above + below) + (fu3[pl.ds(at - 1, span), :] + fu3[pl.ds(at + 1, span), :])
+                    part = around + (ffl[pl.ds(at, span), :] - 0.8 * here) / ffw[pl.ds(at, span), :]
+                    total = part if total is None else total + part
+                    above, here = here, below
+                tmp[pl.ds(pl.multiple_of(n * wx + low - PAD, 8), span), :] = total
             return carry
 
         lax.fori_loop(0, cy, row, 0)
 
     whole = ((PAD, PAD + nx),)
-    sweep(fu0, fu1, ffl, ffw, wx, 1, ry - 2, whole)
-    sweep(fu1, fu2, ffl, ffw, wx, 2, ry - 4, whole)
-    sweep(fu2, fu3, ffl, ffw, wx, 3, ry - 6, whole)
-    defect_rows(PAD + 8, nx - 16)
+    sweep(fu0, fu1, ffl, ffw, wx, 1, ry - 2, whole, None, 7)
+    sweep(fu1, fu2, ffl, ffw, wx, 1, ry - 2, whole, None, 7)
+    sweep(fu2, fu3, ffl, ffw, wx, 1, ry - 2, whole, None, 7)
+    defect_rows(((PAD + 8, PAD + nx - 8),))
 
     for copy in x_copies:
         copy.wait_recv()
@@ -227,11 +233,10 @@
             if t == 2:
                 new = new + rx[side, 2] * column(fu0, near)
             held[side, t + 1, inner] = new
-        sweep(fine[t], fine[t + 1], ffl, ffw, wx, 1, ry - 2, edges, None, 10 if (ry - 2) % 10 == 0 else 2)
+        sweep(fine[t], fine[t + 1], ffl, ffw, wx, 1, ry - 2, edges, None, 14)
     for side, (halo, near) in enumerate(lanes_of):
         fu3[pl.ds(halo, ry, stride=wx), :] = held[side, BEFORE, inner]
-    for low, high in edges:
-        defect_rows(low, high - low)
+    defect_rows(edges)
 
     h_copies = []
 
@@ -271,7 +276,7 @@
         reach = INNER + 1 - t
         low = (CPAD - reach) // 8 * 8
         high = -((-(CPAD + cx + reach)) // 8) * 8
-        sweep(now, later, fc0, fcw, cwx, CPAD - reach, cy + 2 * reach, ((low, high),))
+        sweep(now, later, fc0, fcw, cwx, CPAD - reach, cy + 2 * reach, ((low, high),), None, 8)
         now, later = later, (fcb if t % 2 == 0 else fca)
 
     for copy in h_copies:
@@ -294,7 +299,7 @@
         return carry
 
     lax.fori_loop(0, cy + 2, correct, 0)
-    sweep(fu3, fu0, ffl, ffw, wx, DEPTH - 1, ny + 2, whole)
+    sweep(fu3, fu0, ffl, ffw, wx, DEPTH - 1, ny + 2, whole, None, 6)
     for side, (halo, near) in enumerate(lanes_of):
         here = column(fu3, halo, DEPTH, ny)
         change = here - held[side, BEFORE, pl.ds(8 + DEPTH, ny)]
@@ -308,7 +313,7 @@
     outs = []
     for piece in range(pieces):
         part = ny // pieces
-        sweep(fu0, None, ffl, ffw, wx, DEPTH + piece * part, part, whole, put)
+        sweep(fu0, None, ffl, ffw, wx, DEPTH + piece * part, part, whole, put, 8)
         at = pl.ds(piece * part, part)
         copy = pltpu.make_async_copy(stage.at[at], out_hbm.at[at], out_sem.at[piece])
         copy.start()
@@ -324,7 +329,7 @@
     f32 = jnp.float32
     ry, wx = ny + 2 * DEPTH, nx + 2 * PAD
     cy, cx = ny // RATIO, nx // RATIO
-    assert ny % 8 == 0 and nx % 8 == 0 and INNER <= min(cy, cx) <= CPAD and layers == 128
+    assert (ry - 2) % 14 == 0 and (ny + 2) % 6 == 0 and ny % 32 == 0 and nx % 8 == 0 and INNER <= min(cy, cx) <= CPAD and layers == 128
     fine = pltpu.VMEM((ry, wx, layers), f32)
     coarse = pltpu.VMEM((cy + 2 * CPAD, cx + 2 * CPAD, layers), f32)
     dma = pltpu.SemaphoreType.DMA

time: 43.6 us -> 41.1 us (0.943)
  Pallas kernels: 40.3 us -> 37.8 us
    pallas_call x1, Pallas kernels: 40.3 us -> 37.8 us  [shards(): pl.pallas_call(functools.partial(kernel, lanes, bands, ny, nx), out_shape...]
where the time goes in v3:
time: 41.1 us; the launch traced here: 41 us
  Pallas kernels  37.8 us (92%)
  local copies, waits for them, and re-layouts  3.16 us (8%)
    pallas_call x1, Pallas kernels, shards(): pl.pallas_call(functools.partial(kernel, lanes, bands, ny, nx), out_shape...  37.8 us
    unnamed x1, local copies, waits for them, and re-layouts  3.16 us

profile of v3, /device:TPU:5, one launch (start us, length us, event | category | flops | bytes accessed | tf_op | source)
XLA Modules:
  0.0 41.0 jit_solution(3363456600542636376)
XLA Ops:
  0.0 37.8 %shard_map.37 = f32[64,64,128]{2,1,0:T(8,128)} custom-call(f32[64,64,128]{2,1,0:T(8,128)} %load_hbm.1, f32[64,64,128]{2,1,0:T(8,128)} %start_hbm.1, f32[64,64,128]{2,1,0:T(8,128)} %rate_hbm.1), custom_call_target="tpu_custom_call" | custom-call | tf_op jit(solution)/shard_map/pallas_call | solution.py:336
  37.8 3.2 %copy.5 = f32[64,64,128]{2,1,0:T(8,128)} copy(f32[64,64,128]{2,1,0:T(8,128)} %shard_map.37) | data formatting | bytes 4194304

commit v4 on v3

--- a/solution.py
+++ b/solution.py
@@ -22,7 +22,7 @@
 def kernel(lanes, bands, ny, nx, load_hbm, start_hbm, rate_hbm, out_hbm,
            u0, u1, u2, u3, fl, fw, ca, cb, c0, cw, tmp, stage,
            sx, rx, line, held, csx, crx, crc, hsx, hrx, hry,
-           in_sem, out_sem, xs, xr, ys, yr, kxs, kxr, kys, kyr, kcs, kcr, hxs, hxr, hys, hyr):
+           in_sem, out_sem, xs, xr, ys, yr, kxs, kxr, kys, kyr, kcs, kcr, ws, wr, hxs, hxr, hys, hyr):
     lane, band = lax.axis_index("lane"), lax.axis_index("band")
     sides = ({"lane": lax.rem(lane + lanes - 1, lanes)}, {"lane": lax.rem(lane + 1, lanes)})
     ends = ({"band": lax.rem(band + bands - 1, bands)}, {"band": lax.rem(band + 1, bands)})
@@ -67,6 +67,16 @@
     def column(ref, col, first=0, count=ry):
         return ref[pl.ds(first * wx + col, count, stride=wx), :]
 
+    x_copies = []
+    wheres = [[PAD + d if side == 0 else PAD + nx - 1 - d for d in range(DEPTH)] for side in range(2)]
+    for side, where in enumerate(wheres):
+        first, second = (0.8 / (4.0 + column(ffw, col, DEPTH, ny)) for col in where[:2])
+        sx[side, 0, pl.ds(8, ny)] = column(fu0, where[0], DEPTH, ny)
+        sx[side, 1, pl.ds(8, ny)] = first
+        sx[side, 2, pl.ds(8, ny)] = first * first * second
+        sx[side, 3, pl.ds(8, ny)] = first * column(fu0, where[1], DEPTH, ny) + first * column(ffl, where[0], DEPTH, ny)
+        x_copies.append(remote(sx.at[side, pl.ds(0, 4), pl.ds(8, ny)], rx.at[1 - side, pl.ds(0, 4), pl.ds(8, ny)], xs.at[side, 0], xr.at[1 - side, 0], sides[side]))
+
     for ref in (fu0, fu1, fu2):
         for col in (PAD - 1, PAD + nx):
             ref[pl.ds(col, ry, stride=wx), :] = jnp.zeros((ry, ref.shape[1]), jnp.float32)
@@ -74,22 +84,15 @@
         copy.wait()
 
     inner = pl.ds(8, ry)
+    reached = pl.ds(8 - DEPTH, ry)
 
     def about(ref):
         return ref[pl.ds(7, ry), :] + ref[pl.ds(9, ry), :]
 
-    x_copies = []
-    kept = []
-    for side in range(2):
-        where = [PAD + d if side == 0 else PAD + nx - 1 - d for d in range(DEPTH)]
+    for side, where in enumerate(wheres):
         values = [column(fu0, col) for col in where]
         weights = [0.8 / (4.0 + column(ffw, col)) for col in where[:3]]
         loads = [weight * column(ffl, col) for weight, col in zip(weights, where)]
-        sx[side, 0] = values[0]
-        sx[side, 1] = weights[0]
-        sx[side, 2] = weights[0] * weights[0] * weights[1]
-        sx[side, 3] = weights[0] * values[1] + loads[0]
-        x_copies.append(remote(sx.at[side, pl.ds(0, 4)], rx.at[1 - side, pl.ds(0, 4)], xs.at[side, 0], xr.at[1 - side, 0], sides[side]))
         for d in range(3):
             line[d, inner] = values[d]
         once = []
@@ -98,10 +101,10 @@
             if d > 0:
                 around = around + values[d - 1]
             once.append(0.2 * values[d] + weights[d] * around + loads[d])
-        sx[side, 4] = weights[0] * once[1] + loads[0]
+        sx[side, 4, reached] = weights[0] * once[1] + loads[0]
         line[3, inner] = once[1]
         twice = 0.2 * once[1] + weights[1] * (about(line.at[3]) + once[0] + once[2]) + loads[1]
-        sx[side, 5] = weights[0] * twice + loads[0]
+        sx[side, 5, reached] = weights[0] * twice + loads[0]
         x_copies.append(remote(sx.at[side, pl.ds(4, 2)], rx.at[1 - side, pl.ds(4, 2)], xs.at[side, 1], xr.at[1 - side, 1], sides[side]))
 
     for copy in ins[6:]:
@@ -148,14 +151,14 @@
         ]
 
     def forward(q, side):
-        return [remote(crx.at[side, q], crc.at[side, q, 1 - end], kcs.at[side, q, end], kcr.at[side, q, 1 - end], ends[end]) for end in range(2)]
+        return [remote(crx.at[side, q], crc.at[side, q, 1 - end], kcs.at[side, q, end], kcr.at[side, q, 1 - end], ends[end]) for end in range(1 if bands == 2 else 2)]
 
     def unpack_coarse(q, dst):
         for side in range(2):
             for d in range(INNER):
                 col = CPAD - 1 - d if side == 0 else CPAD + cx + d
                 dst[pl.ds(CPAD * cwx + col, cy, stride=cwx), :] = crx[side, q, d]
-                dst[pl.ds((CPAD - cy) * cwx + col, cy, stride=cwx), :] = crc[side, q, 0, d]
+                dst[pl.ds((CPAD - cy) * cwx + col, cy, stride=cwx), :] = crc[side, q, 1 if bands == 2 else 0, d]
                 dst[pl.ds((CPAD + cy) * cwx + col, cy, stride=cwx), :] = crc[side, q, 1, d]
 
     mass_x = send_coarse(0, fcw)
@@ -218,20 +221,27 @@
     sweep(fu2, fu3, ffl, ffw, wx, 1, ry - 2, whole, None, 7)
     defect_rows(((PAD + 8, PAD + nx - 8),))
 
-    for copy in x_copies:
+    corners = []
+    for side in range(2):
+        x_copies[1 - side].wait_recv()
+        for end, (take, give) in enumerate(((8, 8 + ny), (ny, 0))):
+            corners.append(remote(rx.at[side, pl.ds(0, 4), pl.ds(take, 8)], rx.at[side, pl.ds(0, 4), pl.ds(give, 8)], ws.at[side, end], wr.at[side, 1 - end], ends[end]))
+    for copy in x_copies[2:]:
         copy.wait_recv()
+    for copy in corners:
+        copy.wait()
     edges = ((PAD, PAD + 8), (PAD + nx - 8, PAD + nx))
     lanes_of = ((PAD - 1, PAD), (PAD + nx, PAD + nx - 1))
     fine = (fu0, fu1, fu2, fu3)
     for t in range(BEFORE):
         for side, (halo, near) in enumerate(lanes_of):
             if t == 0:
-                held[side, 0, inner] = rx[side, 0]
+                held[side, 0, inner] = rx[side, 0, reached]
             here = held[side, t, inner]
             fine[t][pl.ds(halo, ry, stride=wx), :] = here
-            new = 0.2 * here + rx[side, 1] * (about(held.at[side, t]) + column(fine[t], near)) + rx[side, 3 + t]
+            new = 0.2 * here + rx[side, 1, reached] * (about(held.at[side, t]) + column(fine[t], near)) + rx[side, 3 + t, reached]
             if t == 2:
-                new = new + rx[side, 2] * column(fu0, near)
+                new = new + rx[side, 2, reached] * column(fu0, near)
             held[side, t + 1, inner] = new
         sweep(fine[t], fine[t + 1], ffl, ffw, wx, 1, ry - 2, edges, None, 14)
     for side, (halo, near) in enumerate(lanes_of):
@@ -304,12 +314,12 @@
         here = column(fu3, halo, DEPTH, ny)
         change = here - held[side, BEFORE, pl.ds(8 + DEPTH, ny)]
         around = column(fu3, halo, DEPTH - 1, ny) + column(fu3, halo, DEPTH + 1, ny) + column(fu3, near, DEPTH, ny) + change
-        fu0[pl.ds(DEPTH * wx + halo, ny, stride=wx), :] = 0.2 * here + rx[side, 1, pl.ds(DEPTH, ny)] * around + hrx[side]
+        fu0[pl.ds(DEPTH * wx + halo, ny, stride=wx), :] = 0.2 * here + rx[side, 1, pl.ds(8, ny)] * around + hrx[side]
 
     def put(y, new):
         stage[y - DEPTH] = new
 
-    pieces = 4
+    pieces = ny // 8
     outs = []
     for piece in range(pieces):
         part = ny // pieces
@@ -342,8 +352,8 @@
             fine, fine, fine, fine, fine, fine, coarse, coarse, coarse, coarse,
             pltpu.VMEM(((cy + 2) * wx, layers), f32),
             pltpu.VMEM((ny, nx, layers), f32),
-            pltpu.VMEM((2, ITEMS, ry, layers), f32),
-            pltpu.VMEM((2, ITEMS, ry, layers), f32),
+            pltpu.VMEM((2, ITEMS, ny + 16, layers), f32),
+            pltpu.VMEM((2, ITEMS, ny + 16, layers), f32),
             pltpu.VMEM((4, ry + 16, layers), f32),
             pltpu.VMEM((2, DEPTH, ry + 16, layers), f32),
             pltpu.VMEM((2, 2, INNER, cy, layers), f32),
@@ -352,9 +362,9 @@
             pltpu.VMEM((2, ny, layers), f32),
             pltpu.VMEM((2, ny, layers), f32),
             pltpu.VMEM((2, nx, layers), f32),
-            dma((3, 3)), dma((4,)),
+            dma((3, 3)), dma((ny // 8,)),
             dma((2, 2)), dma((2, 2)), dma((3, 3, 2)), dma((3, 3, 2)),
-            dma((2, 2)), dma((2, 2)), dma((2, 2)), dma((2, 2)), dma((2, 2, 2)), dma((2, 2, 2)),
+            dma((2, 2)), dma((2, 2)), dma((2, 2)), dma((2, 2)), dma((2, 2, 2)), dma((2, 2, 2)), dma((2, 2)), dma((2, 2)),
             dma((2,)), dma((2,)), dma((2,)), dma((2,)),
         ],
         compiler_params=pltpu.CompilerParams(collective_id=0, has_side_effects=True, vmem_limit_bytes=60 * 2**20),

time: 41.1 us -> 39 us (0.949)
  Pallas kernels: 37.8 us -> 35.7 us
    pallas_call x1, Pallas kernels: 37.8 us -> 35.7 us  [shards(): pl.pallas_call(functools.partial(kernel, lanes, bands, ny, nx), out_shape...]
where the time goes in v4:
time: 39 us; the launch traced here: 38.9 us
  Pallas kernels  35.7 us (92%)
  local copies, waits for them, and re-layouts  3.16 us (8%)
    pallas_call x1, Pallas kernels, shards(): pl.pallas_call(functools.partial(kernel, lanes, bands, ny, nx), out_shape...  35.7 us
    unnamed x1, local copies, waits for them, and re-layouts  3.16 us

profile of v4, /device:TPU:5, one launch (start us, length us, event | category | flops | bytes accessed | tf_op | source)
XLA Modules:
  0.0 38.9 jit_solution(17688068381002062946)
XLA Ops:
  0.0 35.7 %shard_map.37 = f32[64,64,128]{2,1,0:T(8,128)} custom-call(f32[64,64,128]{2,1,0:T(8,128)} %load_hbm.1, f32[64,64,128]{2,1,0:T(8,128)} %start_hbm.1, f32[64,64,128]{2,1,0:T(8,128)} %rate_hbm.1), custom_call_target="tpu_custom_call" | custom-call | tf_op jit(solution)/shard_map/pallas_call | solution.py:346
  35.7 3.2 %copy.5 = f32[64,64,128]{2,1,0:T(8,128)} copy(f32[64,64,128]{2,1,0:T(8,128)} %shard_map.37) | data formatting | bytes 4194304

commit v5 on v4

--- a/solution.py
+++ b/solution.py
@@ -134,13 +134,17 @@
 
     lax.fori_loop(0, cy, mass_row, 0)
 
-    def send_coarse(q, src):
+    parts = ((0, 0, INNER), (1, 2, INNER), (1, 0, 2))
+
+    def send_coarse(part, src):
+        q, shallow, deep = parts[part]
+        span = pl.ds(shallow, deep - shallow)
         copies = []
         for side in range(2):
-            for d in range(INNER):
+            for d in range(shallow, deep):
                 col = d if side == 0 else cx - 1 - d
                 csx[side, q, d] = src[pl.ds(CPAD * cwx + CPAD + col, cy, stride=cwx), :]
-            copies.append(remote(csx.at[side, q], crx.at[1 - side, q], kxs.at[side, q], kxr.at[1 - side, q], sides[side]))
+            copies.append(remote(csx.at[side, q, span], crx.at[1 - side, q, span], kxs.at[side, part], kxr.at[1 - side, part], sides[side]))
         return copies
 
     def send_rows(q, ref):
@@ -150,16 +154,28 @@
             remote(mine, ref.at[pl.ds(CPAD - cy, cy), pl.ds(CPAD, cx)], kys.at[1, q], kyr.at[0, q], ends[1]),
         ]
 
-    def forward(q, side):
-        return [remote(crx.at[side, q], crc.at[side, q, 1 - end], kcs.at[side, q, end], kcr.at[side, q, 1 - end], ends[end]) for end in range(1 if bands == 2 else 2)]
-
-    def unpack_coarse(q, dst):
+    def forward(part, side):
+        q, shallow, deep = parts[part]
+        span = pl.ds(shallow, deep - shallow)
+        return [remote(crx.at[side, q, span], crc.at[side, q, 1 - end, span], kcs.at[side, part, end], kcr.at[side, part, 1 - end], ends[end]) for end in range(1 if bands == 2 else 2)]
+
+    def unpack_coarse(part, dst):
+        q, shallow, deep = parts[part]
         for side in range(2):
-            for d in range(INNER):
+            for d in range(shallow, deep):
                 col = CPAD - 1 - d if side == 0 else CPAD + cx + d
                 dst[pl.ds(CPAD * cwx + col, cy, stride=cwx), :] = crx[side, q, d]
                 dst[pl.ds((CPAD - cy) * cwx + col, cy, stride=cwx), :] = crc[side, q, 1 if bands == 2 else 0, d]
                 dst[pl.ds((CPAD + cy) * cwx + col, cy, stride=cwx), :] = crc[side, q, 1, d]
+
+    def take_coarse(part, copies, dst):
+        forwards = []
+        for side in range(2):
+            copies[1 - side].wait_recv()
+            forwards += forward(part, side)
+        for copy in forwards:
+            copy.wait()
+        unpack_coarse(part, dst)
 
     mass_x = send_coarse(0, fcw)
     mass_y = send_rows(0, cw)
@@ -221,6 +237,13 @@
     sweep(fu2, fu3, ffl, ffw, wx, 1, ry - 2, whole, None, 7)
     defect_rows(((PAD + 8, PAD + nx - 8),))
 
+    def load_row(n, carry):
+        fc0[coarse_at(n), :] = fcw[coarse_at(n), :] * across(n)
+        return carry
+
+    lax.fori_loop(0, cy, load_row, 0)
+    far_x = send_coarse(1, fc0)
+
     corners = []
     for side in range(2):
         x_copies[1 - side].wait_recv()
@@ -250,13 +273,9 @@
 
     h_copies = []
 
-    def load_row(n, carry):
-        fc0[coarse_at(n), :] = fcw[coarse_at(n), :] * across(n)
-        return carry
-
     lax.fori_loop(0, cy, load_row, 0)
 
-    load_x = send_coarse(1, fc0)
+    load_x = send_coarse(2, fc0)
     load_y = send_rows(1, c0)
     for side in range(2):
         col, second = (PAD, PAD + 1) if side == 0 else (PAD + nx - 1, PAD + nx - 2)
@@ -266,20 +285,13 @@
         remote(u3.at[DEPTH + 1, own[1]], hry.at[1], hys.at[0], hyr.at[1], ends[0]),
         remote(u3.at[DEPTH + ny - 2, own[1]], hry.at[0], hys.at[1], hyr.at[0], ends[1]),
     ]
-    forwards = []
-    for side in range(2):
-        mass_x[1 - side].wait_recv()
-        forwards += forward(0, side)
-    for copy in mass_y + forwards:
-        copy.wait()
-    unpack_coarse(0, fcw)
-    forwards = []
-    for side in range(2):
-        load_x[1 - side].wait_recv()
-        forwards += forward(1, side)
-    for copy in load_y + forwards:
-        copy.wait()
-    unpack_coarse(1, fc0)
+    for copy in mass_y:
+        copy.wait()
+    take_coarse(0, mass_x, fcw)
+    take_coarse(1, far_x, fc0)
+    for copy in load_y:
+        copy.wait()
+    take_coarse(2, load_x, fc0)
 
     now, later = fc0, fca
     for t in range(2, INNER + 1):
@@ -328,7 +340,7 @@
         copy = pltpu.make_async_copy(stage.at[at], out_hbm.at[at], out_sem.at[piece])
         copy.start()
         outs.append(copy)
-    for copy in x_copies + mass_x + load_x + h_copies:
+    for copy in x_copies + mass_x + far_x + load_x + h_copies:
         copy.wait_send()
     for copy in outs:
         copy.wait()
@@ -364,7 +376,7 @@
             pltpu.VMEM((2, nx, layers), f32),
             dma((3, 3)), dma((ny // 8,)),
             dma((2, 2)), dma((2, 2)), dma((3, 3, 2)), dma((3, 3, 2)),
-            dma((2, 2)), dma((2, 2)), dma((2, 2)), dma((2, 2)), dma((2, 2, 2)), dma((2, 2, 2)), dma((2, 2)), dma((2, 2)),
+            dma((2, 3)), dma((2, 3)), dma((2, 2)), dma((2, 2)), dma((2, 3, 2)), dma((2, 3, 2)), dma((2, 2)), dma((2, 2)),
             dma((2,)), dma((2,)), dma((2,)), dma((2,)),
         ],
         compiler_params=pltpu.CompilerParams(collective_id=0, has_side_effects=True, vmem_limit_bytes=60 * 2**20),

time: 39 us -> 35.2 us (0.903)
  the two profiles are of different devices: /device:TPU:5 before, /device:TPU:0 now
where the time goes in v5:
time: 35.2 us; the launch traced here: 35.1 us
  Pallas kernels  31.9 us (91%)
  local copies, waits for them, and re-layouts  3.16 us (9%)
    pallas_call x1, Pallas kernels, shards(): pl.pallas_call(functools.partial(kernel, lanes, bands, ny, nx), out_shape...  31.9 us
    unnamed x1, local copies, waits for them, and re-layouts  3.16 us

profile of v5, /device:TPU:0, one launch (start us, length us, event | category | flops | bytes accessed | tf_op | source)
XLA Modules:
  0.0 35.1 jit_solution(4232070793906466384)
XLA Ops:
  0.0 31.9 %shard_map.37 = f32[64,64,128]{2,1,0:T(8,128)} custom-call(f32[64,64,128]{2,1,0:T(8,128)} %load_hbm.1, f32[64,64,128]{2,1,0:T(8,128)} %start_hbm.1, f32[64,64,128]{2,1,0:T(8,128)} %rate_hbm.1), custom_call_target="tpu_custom_call" | custom-call | tf_op jit(solution)/shard_map/pallas_call | solution.py:358
  31.9 3.2 %copy.5 = f32[64,64,128]{2,1,0:T(8,128)} copy(f32[64,64,128]{2,1,0:T(8,128)} %shard_map.37) | data formatting | bytes 4194304
